TPU v7x, 32 devices: a whole 2x2x4 slice. The times are simulated.
32 devices in a mesh: slab: 8 (over z, y), sub: 4 (over x, core).
Axes of the slice: x: 2, y: 2, z: 4, core: 2. Of those that a mesh axis runs over, the one named last changes fastest.
Arguments:
- factor_obs: float32 [32, 64, 64, 512], P('slab', 'sub'), may hold values from -0.20992233 to 0.20992233
- factor_ctrl: float32 [32, 64, 64, 512], P('slab', 'sub'), may hold values from -0.20992233 to 0.20992233
- diffusivity: float32 [32, 4096], P('slab', 'sub'), may hold values from 0.5 to 2
- input_map: float32 [4, 32, 4096], P(None, 'slab', 'sub'), may hold values from -2 to 2
- output_map: float32 [4, 32, 4096], P(None, 'slab', 'sub'), may hold values from -2 to 2
- start_block: float32 [512, 128], replicated, may hold values from -6 to 6
- order: int32 [1], replicated, may hold values from 64 to 128
Outputs:
- reduced_mass: float32 [128, 128], replicated
- reduced_state: float32 [128, 128], replicated
- reduced_input: float32 [128, 4], replicated
- reduced_output: float32 [4, 128], replicated
All inputs are finite; a program needn't handle non-finite values.
Results may differ from a plain program's by a relative error of at most 0.00017.
Values sent between devices are 32-bit elements; how exact they have to be, the bound alone decides.
A program may use at most 128 MiB of HBM per device.

v0:
```python
import functools
import jax
import jax.numpy as jnp
from jax import lax
from jax.experimental import pallas as pl
from jax.experimental.pallas import tpu as pltpu
from jax.sharding import PartitionSpec as P

LANES = 128
PANEL = 8
HIGHEST = lax.Precision.HIGHEST
HIGH = lax.Precision.HIGH


def exact(first, second, dims=((1,), (0,))):
    return lax.dot_general(
        first, second, (dims, ((), ())), precision=HIGHEST, preferred_element_type=jnp.float32
    )


def tall(first, second, dims=((1,), (0,))):
    return lax.dot_general(
        first, second, (dims, ((), ())), precision=HIGH, preferred_element_type=jnp.float32
    )


def narrow(first, second, dims=((1,), (0,))):
    return lax.dot_general(first, second, (dims, ((), ())), preferred_element_type=jnp.float32)


def three_parts(value):
    high = value.astype(jnp.bfloat16).astype(jnp.float32)
    mid = (value - high).astype(jnp.bfloat16).astype(jnp.float32)
    return high, mid, value - high - mid


def two_parts(value):
    high = value.astype(jnp.bfloat16)
    return high, (value - high.astype(jnp.float32)).astype(jnp.bfloat16)


def three_dots(first, second, dims=((1,), (0,))):
    (a, b), (c, d) = two_parts(first), two_parts(second)
    return narrow(a, c, dims) + (narrow(a, d, dims) + narrow(b, c, dims))


def gram_kernel(first_ref, second_ref, out_ref):
    @pl.when(pl.program_id(0) == 0)
    def _():
        out_ref[...] = jnp.zeros_like(out_ref)

    out_ref[...] += three_dots(first_ref[...], second_ref[...], ((0,), (0,)))


def cells_step(cells):
    return 512 if cells % 512 == 0 else cells


def gram(first, second):
    cells, wide = first.shape
    step = cells_step(cells)
    spec = pl.BlockSpec((step, wide), lambda k: (k, 0))
    return pl.pallas_call(
        gram_kernel,
        grid=(cells // step,),
        out_shape=jax.ShapeDtypeStruct((wide, second.shape[1]), jnp.float32),
        in_specs=[spec, spec],
        out_specs=pl.BlockSpec((wide, second.shape[1]), lambda k: (0, 0)),
        compiler_params=pltpu.CompilerParams(dimension_semantics=("arbitrary",)),
    )(first, second)


def sub_bits(count):
    return [1 << b for b in range(count.bit_length() - 1)]


def all_reduce_kernel(nslab, nsub, in_ref, out_ref, work, got_sub, got_slab, *sems):
    rs_sub_send, rs_sub_recv, rs_slab_send, rs_slab_recv = sems[:4]
    ag_slab_send, ag_slab_recv, ag_sub_send, ag_sub_recv = sems[4:]
    slab, sub = lax.axis_index("slab"), lax.axis_index("sub")
    rows, cols = work.shape[0], in_ref.shape[1]
    bits = sub_bits(nsub)

    def partner(bit):
        has = lax.rem(sub // bit, 2)
        return has, sub + bit - 2 * bit * has

    barrier = pltpu.get_barrier_semaphore()
    for bit in bits:
        pl.semaphore_signal(barrier, inc=1, device_id={"sub": partner(bit)[1]})
    for off in range(1, nslab):
        pl.semaphore_signal(barrier, inc=1, device_id={"slab": lax.rem(slab + off, nslab)})

    tall_rows = in_ref.shape[0]
    for c in range(cols // LANES):
        work[c * tall_rows : (c + 1) * tall_rows, :] = in_ref[:, c * LANES : (c + 1) * LANES]
    pl.semaphore_wait(barrier, len(bits) + nslab - 1)

    base, length, taken = 0, rows, 0
    for s, bit in enumerate(bits):
        half = length // 2
        has, other = partner(bit)
        keep = pl.multiple_of(base + has * half, 8)
        give = pl.multiple_of(base + (1 - has) * half, 8)
        copy = pltpu.make_async_remote_copy(
            src_ref=work.at[pl.ds(give, half)],
            dst_ref=got_sub.at[pl.ds(taken, half)],
            send_sem=rs_sub_send.at[s],
            recv_sem=rs_sub_recv.at[s],
            device_id={"sub": other},
        )
        copy.start()
        copy.wait()
        work[pl.ds(keep, half), :] += got_sub[taken : taken + half, :]
        base, length, taken = keep, half, taken + half

    piece = length // nslab
    copies = []
    for off in range(1, nslab):
        peer = lax.rem(slab + off, nslab)
        copy = pltpu.make_async_remote_copy(
            src_ref=work.at[pl.ds(pl.multiple_of(base + peer * piece, 8), piece)],
            dst_ref=got_slab.at[off],
            send_sem=rs_slab_send.at[off],
            recv_sem=rs_slab_recv.at[off],
            device_id={"slab": peer},
        )
        copy.start()
        copies.append(copy)
    mine = pl.multiple_of(base + slab * piece, 8)
    total = work[pl.ds(mine, piece), :]
    for off in range(1, nslab):
        copies[off - 1].wait_recv()
        total = total + got_slab[off]
    out_ref[pl.ds(mine, piece), :] = total
    for copy in copies:
        copy.wait_send()

    copies = []
    for off in range(1, nslab):
        copy = pltpu.make_async_remote_copy(
            src_ref=out_ref.at[pl.ds(mine, piece)],
            dst_ref=out_ref.at[pl.ds(mine, piece)],
            send_sem=ag_slab_send.at[off],
            recv_sem=ag_slab_recv.at[off],
            device_id={"slab": lax.rem(slab + off, nslab)},
        )
        copy.start()
        copies.append(copy)
    for copy in copies:
        copy.wait()

    for s in reversed(range(len(bits))):
        has, other = partner(bits[s])
        copy = pltpu.make_async_remote_copy(
            src_ref=out_ref.at[pl.ds(base, length)],
            dst_ref=out_ref.at[pl.ds(base, length)],
            send_sem=ag_sub_send.at[s],
            recv_sem=ag_sub_recv.at[s],
            device_id={"sub": other},
        )
        copy.start()
        copy.wait()
        base = pl.multiple_of(base - has * length, 8)
        length = 2 * length


def all_reduce(part, ident):
    nslab, nsub = lax.axis_size("slab"), lax.axis_size("sub")
    rows = part.shape[0] * (part.shape[1] // LANES)
    bits = len(sub_bits(nsub))
    piece = rows // (nsub * nslab)
    sub_sem, slab_sem = pltpu.SemaphoreType.DMA((bits,)), pltpu.SemaphoreType.DMA((nslab,))
    return pl.pallas_call(
        functools.partial(all_reduce_kernel, nslab, nsub),
        out_shape=jax.ShapeDtypeStruct((rows, LANES), jnp.float32),
        in_specs=[pl.BlockSpec(memory_space=pltpu.VMEM)],
        out_specs=pl.BlockSpec(memory_space=pltpu.VMEM),
        scratch_shapes=[
            pltpu.VMEM((rows, LANES), jnp.float32),
            pltpu.VMEM((rows, LANES), jnp.float32),
            pltpu.VMEM((nslab, piece, LANES), jnp.float32),
            sub_sem, sub_sem, slab_sem, slab_sem, slab_sem, slab_sem, sub_sem, sub_sem,
        ],
        compiler_params=pltpu.CompilerParams(collective_id=ident, has_side_effects=True),
    )(part)


def small_kernel(nslab, nsub, in_ref, out_ref, total, slots, got_slab, *sems):
    sub_send, sub_recv, rs_send, rs_recv, ag_send, ag_recv = sems
    slab, sub = lax.axis_index("slab"), lax.axis_index("sub")
    barrier = pltpu.get_barrier_semaphore()
    for off in range(1, nsub):
        pl.semaphore_signal(barrier, inc=1, device_id={"sub": lax.rem(sub + off, nsub)})
    for off in range(1, nslab):
        pl.semaphore_signal(barrier, inc=1, device_id={"slab": lax.rem(slab + off, nslab)})
    pl.semaphore_wait(barrier, nsub + nslab - 2)

    copies = []
    for off in range(1, nsub):
        copy = pltpu.make_async_remote_copy(
            src_ref=in_ref,
            dst_ref=slots.at[sub],
            send_sem=sub_send.at[off],
            recv_sem=sub_recv.at[off],
            device_id={"sub": lax.rem(sub + off, nsub)},
        )
        copy.start()
        copies.append(copy)
    slots[sub] = in_ref[...]
    for copy in copies:
        copy.wait()
    value = slots[0]
    for k in range(1, nsub):
        value = value + slots[k]
    total[...] = value

    piece = in_ref.shape[0] // nslab
    copies = []
    for off in range(1, nslab):
        peer = lax.rem(slab + off, nslab)
        copy = pltpu.make_async_remote_copy(
            src_ref=total.at[pl.ds(pl.multiple_of(peer * piece, 8), piece)],
            dst_ref=got_slab.at[off],
            send_sem=rs_send.at[off],
            recv_sem=rs_recv.at[off],
            device_id={"slab": peer},
        )
        copy.start()
        copies.append(copy)
    mine = pl.multiple_of(slab * piece, 8)
    value = total[pl.ds(mine, piece), :]
    for off in range(1, nslab):
        copies[off - 1].wait()
        value = value + got_slab[off]
    out_ref[pl.ds(mine, piece), :] = value
    copies = []
    for off in range(1, nslab):
        copy = pltpu.make_async_remote_copy(
            src_ref=out_ref.at[pl.ds(mine, piece)],
            dst_ref=out_ref.at[pl.ds(mine, piece)],
            send_sem=ag_send.at[off],
            recv_sem=ag_recv.at[off],
            device_id={"slab": lax.rem(slab + off, nslab)},
        )
        copy.start()
        copies.append(copy)
    for copy in copies:
        copy.wait()


def small_all_reduce(part, ident):
    nslab, nsub = lax.axis_size("slab"), lax.axis_size("sub")
    rows = part.shape[0]
    sub_sem, slab_sem = pltpu.SemaphoreType.DMA((nsub,)), pltpu.SemaphoreType.DMA((nslab,))
    return pl.pallas_call(
        functools.partial(small_kernel, nslab, nsub),
        out_shape=jax.ShapeDtypeStruct((rows, LANES), jnp.float32),
        in_specs=[pl.BlockSpec(memory_space=pltpu.VMEM)],
        out_specs=pl.BlockSpec(memory_space=pltpu.VMEM),
        scratch_shapes=[
            pltpu.VMEM((rows, LANES), jnp.float32),
            pltpu.VMEM((nsub, rows, LANES), jnp.float32),
            pltpu.VMEM((nslab, rows // nslab, LANES), jnp.float32),
            sub_sem, sub_sem, slab_sem, slab_sem, slab_sem, slab_sem,
        ],
        compiler_params=pltpu.CompilerParams(collective_id=ident, has_side_effects=True),
    )(part)


def inverse_factor(work, size):
    for base in range(0, size, PANEL):
        rows = [
            jnp.broadcast_to(work[base + i : base + i + 1, :], (PANEL, 2 * size))
            for i in range(PANEL)
        ]
        block = [
            [
                jnp.broadcast_to(rows[i][:, base + j : base + j + 1], (PANEL, LANES))
                if j >= i
                else None
                for j in range(PANEL)
            ]
            for i in range(PANEL)
        ]
        wide = 2 * size // LANES
        for j in range(PANEL):
            scale = lax.rsqrt(block[j][j])
            lead = [block[j][i] * scale if i > j else None for i in range(PANEL)]
            rows[j] = rows[j] * jnp.concatenate([scale] * wide, axis=1)
            for i in range(j + 1, PANEL):
                for m in range(i, PANEL):
                    block[i][m] = block[i][m] - lead[i] * lead[m]
                rows[i] = rows[i] - jnp.concatenate([lead[i]] * wide, axis=1) * rows[j]
        place = lax.broadcasted_iota(jnp.int32, (PANEL, 2 * size), 0)
        panel = rows[0]
        for i in range(1, PANEL):
            panel = jnp.where(place == i, rows[i], panel)
        work[base : base + PANEL, :] = panel
        if base + PANEL < size:
            high, mid, low = three_parts(panel)
            first = jnp.concatenate([high, high, mid, high, low, mid], axis=0)[:, :size]
            second = jnp.concatenate([high, mid, high, low, high, mid], axis=0)
            update = narrow(first.astype(jnp.bfloat16), second.astype(jnp.bfloat16), ((0,), (0,)))
            work[base + PANEL :, :] = work[base + PANEL :, :] - update[base + PANEL :, :]


def bases_kernel(sweeps, gram_ref, start_ref, left_ref, right_ref, mass_ref, both, block, work):
    rank, size = start_ref.shape
    for c in range(rank // LANES):
        cols = slice(c * LANES, (c + 1) * LANES)
        tile = gram_ref[c * rank : (c + 1) * rank, :]
        both[1, :, cols] = tile
        both[0, cols, :] = tile.T
    block[...] = start_ref[...]
    row = lax.broadcasted_iota(jnp.int32, (size, size), 0)
    col = lax.broadcasted_iota(jnp.int32, (size, size), 1)
    eye = (row == col).astype(jnp.float32)

    def step(k, carry):
        product = exact(both[lax.rem(k, 2)], block[...])
        work[:, :size] = exact(product, product, ((0,), (0,)))
        work[:, size:] = eye
        inverse_factor(work, size)
        right_ref[...] = left_ref[...]
        basis = exact(product, work[:, size:], ((1,), (1,)))
        block[...] = basis
        left_ref[...] = basis
        return carry

    left_ref[...] = start_ref[...]
    lax.fori_loop(0, 2 * sweeps, step, 0)
    mass_ref[...] = exact(left_ref[...], exact(both[1], right_ref[...]), ((0,), (0,)))


def subspace_bases(cross_gram, start_block):
    rank, size = start_block.shape
    tall_shape = jax.ShapeDtypeStruct((rank, size), jnp.float32)
    vmem = pl.BlockSpec(memory_space=pltpu.VMEM)
    return pl.pallas_call(
        functools.partial(bases_kernel, 2),
        out_shape=(tall_shape, tall_shape, jax.ShapeDtypeStruct((size, size), jnp.float32)),
        in_specs=[vmem, vmem],
        out_specs=(vmem, vmem, vmem),
        scratch_shapes=[
            pltpu.VMEM((2, rank, rank), jnp.float32),
            pltpu.VMEM((rank, size), jnp.float32),
            pltpu.VMEM((size, 2 * size), jnp.float32),
        ],
    )(cross_gram, start_block)


def block_order(k, count, per_plane):
    inner = jnp.where(k < 2 * per_plane, count - 2 * per_plane + k, k - per_plane)
    return jnp.where(k < per_plane, k, inner)


def project_kernel(nslab, nsub, per_plane, *refs):
    ctrl_cells, obs_cells, right_ref, left_ref, ctrl_ref, obs_ref = refs[:6]
    faces, halves, landed, (send, recv) = refs[6:10], refs[10], refs[11:15], refs[15:]
    k = pl.program_id(0)
    count = pl.num_programs(0) // 2
    planes, lines, points, size = ctrl_ref.shape
    slab, sub = lax.axis_index("slab"), lax.axis_index("sub")
    moves = (
        ("slab", slab, nslab, 1, ctrl_ref.at[planes - 1]),
        ("slab", slab, nslab, -1, ctrl_ref.at[0]),
        ("sub", sub, nsub, 1, ctrl_ref.at[:, lines - 1]),
        ("sub", sub, nsub, -1, ctrl_ref.at[:, 0]),
    )

    def there(me, total, step):
        return me < total - 1 if step > 0 else me > 0

    def copy(m):
        axis, me, _, step, source = moves[m]
        return pltpu.make_async_remote_copy(
            src_ref=source,
            dst_ref=landed[m],
            send_sem=send.at[m],
            recv_sem=recv.at[m],
            device_id={axis: me + step},
        )

    def each(picked, act):
        for m in picked:
            _, me, total, step, _ = moves[m]

            @pl.when(there(me, total, step))
            def _():
                act(m)

    def product(cells, which):
        high, low = two_parts(cells)
        wide = narrow(high, halves[which])
        return wide[:, :size] + (wide[:, size:] + narrow(low, halves[which, :, :size]))

    @pl.when(k == 0)
    def _():
        barrier = pltpu.get_barrier_semaphore()
        for axis, me, total, step, _ in moves:
            beside = lax.rem(me + step + total, total)
            pl.semaphore_signal(barrier, inc=1, device_id={axis: beside})
        pl.semaphore_wait(barrier, len(moves))
        for which, basis in enumerate((right_ref, left_ref)):
            high, low = two_parts(basis[...])
            halves[which, :, :size] = high
            halves[which, :, size:] = low

    @pl.when(k < count)
    def _():
        block = block_order(k, count, per_plane)
        some = lines // per_plane
        value = product(ctrl_cells[...], 0).reshape(some, points, size)
        ctrl_ref[block // per_plane, pl.ds(lax.rem(block, per_plane) * some, some)] = value

    @pl.when(k >= count)
    def _():
        obs_ref[...] = product(obs_cells[...], 1)

    @pl.when(k == 2 * per_plane - 1)
    def _():
        each((0, 1), lambda m: copy(m).start())

    @pl.when(k == count - 1)
    def _():
        each((2, 3), lambda m: copy(m).start())

    @pl.when(k == 2 * count - 1)
    def _():
        for m, (_, me, total, step, _) in enumerate(moves):

            @pl.when(there(me, total, step))
            def _():
                copy(m).wait_send()

            @pl.when(there(me, total, -step))
            def _():
                copy(m).wait_recv()
                faces[m][...] = landed[m][...]

            @pl.when(jnp.logical_not(there(me, total, -step)))
            def _():
                faces[m][...] = jnp.zeros(landed[m].shape, jnp.float32)


def project(factor_ctrl, factor_obs, right_basis, left_basis, ident):
    nslab, nsub = lax.axis_size("slab"), lax.axis_size("sub")
    planes, lines, points, wide = factor_ctrl.shape
    cells, size = planes * lines * points, right_basis.shape[1]
    per_plane = 2 if lines % 2 == 0 else 1
    count, step = planes * per_plane, lines * points // per_plane
    shapes = [(lines, points, size)] * 2 + [(planes, points, size)] * 2
    grid_shape = (planes, lines, points, size)
    four = pltpu.SemaphoreType.DMA((4,))
    basis_spec = pl.BlockSpec((wide, size), lambda k: (0, 0))
    return pl.pallas_call(
        functools.partial(project_kernel, nslab, nsub, per_plane),
        grid=(2 * count,),
        out_shape=[
            jax.ShapeDtypeStruct(grid_shape, jnp.float32),
            jax.ShapeDtypeStruct((cells, size), jnp.float32),
        ]
        + [jax.ShapeDtypeStruct(shape, jnp.float32) for shape in shapes],
        in_specs=[
            pl.BlockSpec(
                (step, wide),
                lambda k: (block_order(jnp.minimum(k, count - 1), count, per_plane), 0),
            ),
            pl.BlockSpec((step, wide), lambda k: (jnp.maximum(k - count, 0), 0)),
            basis_spec,
            basis_spec,
        ],
        out_specs=[
            pl.BlockSpec(grid_shape, lambda k: (0, 0, 0, 0)),
            pl.BlockSpec((step, size), lambda k: (jnp.maximum(k - count, 0), 0)),
        ]
        + [pl.BlockSpec(shape, lambda k: (0, 0, 0)) for shape in shapes],
        scratch_shapes=[pltpu.VMEM((2, wide, 2 * size), jnp.bfloat16)]
        + [pltpu.VMEM(shape, jnp.float32) for shape in shapes]
        + [four, four],
        compiler_params=pltpu.CompilerParams(
            collective_id=ident,
            has_side_effects=True,
            dimension_semantics=("arbitrary",),
        ),
    )(factor_ctrl.reshape(cells, wide), factor_obs.reshape(cells, wide), right_basis, left_basis)


def on_device(factor_obs, factor_ctrl, diffusivity, input_map, output_map, start_block, order):
    planes, lines, points, rank = factor_ctrl.shape
    cells = planes * lines * points
    size = start_block.shape[1]
    observe = factor_obs.reshape(cells, rank)
    control = factor_ctrl.reshape(cells, rank)
    conduct = diffusivity.reshape(planes, lines, points)
    drive = input_map.reshape(input_map.shape[0], cells)
    sense = output_map.reshape(output_map.shape[0], cells)
    ins, outs = drive.shape[0], sense.shape[0]

    cross_gram = all_reduce(gram(observe, control), 0)
    left_basis, right_basis, mass = subspace_bases(cross_gram, start_block)

    ctrl, obs_space, below, above, before, after = project(
        factor_ctrl, factor_obs, right_basis, left_basis, 2
    )
    ctrl_flat = ctrl.reshape(cells, size)
    below, above = below[None], above[None]
    before, after = before[:, None], after[:, None]
    zs = jnp.concatenate([below, ctrl, above], axis=0)
    ys = jnp.concatenate([before, ctrl, after], axis=1)
    xs = jnp.pad(ctrl, ((0, 0), (0, 0), (1, 1), (0, 0)))
    beside = zs[2:] + zs[:-2] + ys[:, 2:] + ys[:, :-2] + xs[:, :, 2:] + xs[:, :, :-2]
    applied = (conduct[..., None] * (beside - 6.0 * ctrl) / 6.0).reshape(cells, size)
    state = tall(obs_space, applied, ((0,), (0,)))
    used = size + ins + outs
    grain = 8 * lax.axis_size("slab")
    packed = jnp.concatenate(
        [
            state,
            tall(drive, obs_space),
            tall(sense, ctrl_flat),
            jnp.zeros((-used % grain, size), jnp.float32),
        ],
        axis=0,
    )
    summed = small_all_reduce(packed, 1)
    kept = (jnp.arange(size, dtype=jnp.int32) < order[0]).astype(jnp.float32)
    square = kept[:, None] * kept[None, :]
    reduced_input = kept[:, None] * summed[size : size + ins].T
    reduced_output = kept[None, :] * summed[size + ins : used]
    return (square * mass, square * summed[:size], reduced_input, reduced_output)


def solution(mesh):
    placed = (
        P("slab", "sub", None, None),
        P("slab", "sub", None, None),
        P("slab", "sub"),
        P(None, "slab", "sub"),
        P(None, "slab", "sub"),
        P(),
        P(),
    )
    return jax.shard_map(
        on_device, mesh=mesh, in_specs=placed, out_specs=(P(), P(), P(), P()), check_vma=False
    )
```

profile of v0, /device:TPU:0, one launch (start us, length us, event | category | flops | bytes accessed | tf_op | source)
XLA Modules:
  0.0 155.2 jit_solution(2652333956970895507)
XLA Ops:
  0.6 12.7 %shard_map.102.in_ref = f32[512,512]{1,0:T(8,128)} custom-call(f32[4096,512]{1,0:T(8,128)} %bitcast.32, f32[4096,512]{1,0:T(8,128)} %bitcast.30), custom_call_target="tpu_custom_call" | custom-call | tf_op jit(solution)/shard_map/pallas_call | solution.py:63
  13.4 37.6 %shard_map.103.gram_ref = f32[2048,128]{1,0:T(8,128)} custom-call(f32[512,512]{1,0:T(8,128)} %shard_map.102.in_ref), custom_call_target="tpu_custom_call" | custom-call | tf_op jit(solution)/shard_map/pallas_call | solution.py:174
  50.9 35.0 %shard_map.104 = (f32[512,128]{1,0:T(8,128)}, f32[512,128]{1,0:T(8,128)}, f32[128,128]{1,0:T(8,128)}) custom-call(f32[2048,128]{1,0:T(8,128)} %shard_map.103.gram_ref, f32[512,128]{1,0:T(8,128)} %start_ref.1), custom_call_target="tpu_custom_call" | custom-call | tf_op jit(solution)/shard_map/pallas_call | solution.py:340
  85.9 33.1 %shard_map.105 = (f32[4,16,64,128]{3,2,1,0:T(8,128)}, f32[4096,128]{1,0:T(8,128)}, f32[16,64,128]{2,1,0:T(8,128)}, f32[16,64,128]{2,1,0:T(8,128)}, f32[4,64,128]{2,1,0:T(8,128)}, /*index=5*/f32[4,64,128]{2,1,0:T(8,128)}) custom-call(f32[4096,512]{1,0:T(8,128)} %bitcast.31, f32[4096,512]{1,0:T(8,128)} %bitcast.33, f32[512,128]{1,0:T(8,128)} %get-tuple-element.14.refs_2_, ...), custom_call_target="tpu_custom_call" | custom-call | tf_op jit(solution)/shard_map/pallas_call | solution.py:457
  119.1 0.0 copy-done.5
  119.1 0.1 mul.53
  119.2 7.4 %fusion.4 = f32[4,16,64,128]{3,2,1,0:T(8,128)S(1)} fusion(f32[4,16,64,128]{3,2,1,0:T(8,128)} %get-tuple-element.17, f32[4,1,64,128]{3,2,1,0:T(8,128)} %bitcast.40, f32[4,1,64,128]{3,2,1,0:T(8,128)} %bitcast.41, f32[1,16,64,128]{3,2,1,0:T(8,128)} %bitcast.36, f32[1,16,64,128]{3,2,1,0:T(8,128)} %bitcast.37, f32[4,16,64]{2,1,0:T(8,128)S(1)} %mul.53), kind=kLoop, calls=%fused_computation.6 | loop fusion | flops 6815744 | bytes 5521408 | tf_op jit(solution)/shard_map/div | solution.py:514
  126.6 0.0 copy-done
  126.6 0.0 copy-start.2
  126.6 0.0 copy-start.1
  126.6 1.9 %fusion.8 = f32[128,128]{1,0:T(8,128)S(1)} fusion(f32[4096,128]{1,0:T(8,128)S(1)} %copy-done, f32[4096,128]{1,0:T(8,128)S(1)} %bitcast.35), kind=kOutput, calls=%fused_computation.22 | convolution fusion | flops 402653184 | bytes 4259840 | tf_op jit(solution)/shard_map/dot_general | solution.py:22
  128.5 0.0 copy-start.3
  128.6 0.0 copy-done.2
  128.6 0.0 copy-done.1
  128.6 0.0 copy-start.4
  128.6 0.6 convolution_bitcast_fusion
  129.2 0.1 copy-done.3
  129.4 0.6 convolution_bitcast_fusion.1
  130.0 0.1 pad.8.clone
  130.1 0.7 maximum_maximum_fusion.in_ref
  130.9 20.7 %shard_map.106 = f32[192,128]{1,0:T(8,128)} custom-call(f32[192,128]{1,0:T(8,128)} %maximum_maximum_fusion.in_ref), custom_call_target="tpu_custom_call" | custom-call | tf_op jit(solution)/shard_map/pallas_call | solution.py:256
  152.3 0.0 copy-done.4
  152.3 1.6 %multiply_multiply_fusion = (f32[128,128]{1,0:T(8,128)}, f32[128,128]{1,0:T(8,128)}) fusion(f32[192,128]{1,0:T(8,128)} %shard_map.106, f32[128]{0:T(128)S(1)} %compare_convert_fusion, f32[128,128]{1,0:T(8,128)S(1)} %copy-done.4), kind=kLoop, calls=%fused_computation.17 | loop fusion | flops 49152 | bytes 263168 | tf_op jit(solution)/shard_map/mul | solution.py:532
  153.9 1.3 slice_multiply_fusion
  (6 shorter events, 0.1 us)
Async XLA Ops:
  85.9 33.2 %copy-start.5 = (f32[4,1024]{1,0:T(4,128)S(1)}, f32[4,1024]{1,0:T(4,128)}, u32[]{:S(2)}) copy-start(f32[4,1024]{1,0:T(4,128)} %param.9) | copy-start | bytes 49156
  119.1 7.4 %copy-start = (f32[4096,128]{1,0:T(8,128)S(1)}, f32[4096,128]{1,0:T(8,128)}, u32[]{:S(2)}) copy-start(f32[4096,128]{1,0:T(8,128)} %get-tuple-element.16) | copy-start | bytes 6291460
  126.6 2.0 %copy-start.2 = (f32[4,4,1024]{2,1,0:T(4,128)S(1)}, f32[4,4,1024]{2,1,0:T(4,128)}, u32[]{:S(2)}) copy-start(f32[4,4,1024]{2,1,0:T(4,128)} %param.11) | copy-start | bytes 196612
  126.6 2.0 %copy-start.1 = (f32[4,16,64,128]{3,2,1,0:T(8,128)S(1)}, f32[4,16,64,128]{3,2,1,0:T(8,128)}, u32[]{:S(2)}) copy-start(f32[4,16,64,128]{3,2,1,0:T(8,128)} %get-tuple-element.17) | copy-start | bytes 6291460
  128.5 0.8 copy-start.3
  128.6 23.6 %copy-start.4 = (f32[128,128]{1,0:T(8,128)S(1)}, f32[128,128]{1,0:T(8,128)}, u32[]{:S(2)}) copy-start(f32[128,128]{1,0:T(8,128)} %get-tuple-element.13) | copy-start | bytes 196612
where the time goes:
time: 156 us; the launch traced here: 155 us
  Pallas kernels  139 us (89%)
  other arithmetic  11.1 us (7%)
  matrix products  3.13 us (2%)
    pallas_call x1, Pallas kernels, all_reduce(): pl.pallas_call(functools.partial(all_reduce_kernel, nslab, nsub), out_sha...  37.6 us
    pallas_call x1, Pallas kernels, subspace_bases(): pl.pallas_call(functools.partial(bases_kernel, 2), out_shape=(tall_shape,...  35 us
    pallas_call x1, Pallas kernels, project(): pl.pallas_call(functools.partial(project_kernel, nslab, nsub, per_plane),...  33.1 us
    pallas_call x1, Pallas kernels, small_all_reduce(): pl.pallas_call(functools.partial(small_kernel, nslab, nsub), out_shape=ja...  20.7 us
    pallas_call x1, Pallas kernels, gram(): pl.pallas_call(gram_kernel, grid=(cells // step,), out_shape=jax.ShapeDty...  12.7 us
    div x1, other arithmetic, on_device(): conduct[..., None] * (beside - 6.0 * ctrl) / 6.0  7.43 us
    dot_general x3, matrix products, tall(): lax.dot_general(first, second, (dims, ((), ())), precision=HIGH, preferre...  3.13 us

commit v1 on v0

--- a/solution.py
+++ b/solution.py
@@ -7,7 +7,8 @@
 from jax.sharding import PartitionSpec as P
 
 LANES = 128
-PANEL = 8
+SUBS = 8
+PANEL = 16
 HIGHEST = lax.Precision.HIGHEST
 HIGH = lax.Precision.HIGH
 
@@ -268,69 +269,129 @@
     )(part)
 
 
+def across(block, sub):
+    return jnp.broadcast_to(block[sub : sub + 1, :], block.shape)
+
+def column(rows, lane):
+    return jnp.broadcast_to(rows[:, lane : lane + 1], (SUBS, LANES))
+
 def inverse_factor(work, size):
+    wide = 2 * size // LANES
+    place = lax.broadcasted_iota(jnp.int32, (SUBS, 2 * size), 0)
+    spread = lambda x: jnp.concatenate([x] * wide, axis=1)
+    carried = [work[h * SUBS : (h + 1) * SUBS, :] for h in range(2)]
     for base in range(0, size, PANEL):
-        rows = [
-            jnp.broadcast_to(work[base + i : base + i + 1, :], (PANEL, 2 * size))
-            for i in range(PANEL)
-        ]
-        block = [
-            [
-                jnp.broadcast_to(rows[i][:, base + j : base + j + 1], (PANEL, LANES))
-                if j >= i
-                else None
-                for j in range(PANEL)
-            ]
-            for i in range(PANEL)
-        ]
-        wide = 2 * size // LANES
+        low, high = carried
+        cols_low = [column(low, base + j) for j in range(SUBS)]
+        cols_high = [column(high, base + j) for j in range(PANEL)]
+        panel_low, panel_high = low, high
+        scales, rows, leads = [], [], []
         for j in range(PANEL):
-            scale = lax.rsqrt(block[j][j])
-            lead = [block[j][i] * scale if i > j else None for i in range(PANEL)]
-            rows[j] = rows[j] * jnp.concatenate([scale] * wide, axis=1)
-            for i in range(j + 1, PANEL):
-                for m in range(i, PANEL):
-                    block[i][m] = block[i][m] - lead[i] * lead[m]
-                rows[i] = rows[i] - jnp.concatenate([lead[i]] * wide, axis=1) * rows[j]
-        place = lax.broadcasted_iota(jnp.int32, (PANEL, 2 * size), 0)
-        panel = rows[0]
-        for i in range(1, PANEL):
-            panel = jnp.where(place == i, rows[i], panel)
+            if j < SUBS:
+                scale = lax.rsqrt(across(cols_low[j], j))
+                lead_low = cols_low[j] * scale
+                row = across(low, j) * spread(scale)
+                panel_low = jnp.where(place == j, row, panel_low)
+            else:
+                scale = lax.rsqrt(across(cols_high[j], j - SUBS))
+                row = across(high, j - SUBS) * spread(scale)
+                panel_high = jnp.where(place == j - SUBS, row, panel_high)
+            lead_high = cols_high[j] * scale
+            lead = {}
+            for m in range(j + 1, PANEL):
+                if m < SUBS:
+                    lead[m] = across(lead_low, m)
+                    cols_low[m] = cols_low[m] - lead_low * lead[m]
+                else:
+                    lead[m] = across(lead_high, m - SUBS)
+                cols_high[m] = cols_high[m] - lead_high * lead[m]
+            if j < SUBS - 1:
+                low = low - spread(lead_low) * row
+            if j < PANEL - 1:
+                high = high - spread(lead_high) * row
+            scales.append(scale)
+            rows.append(row)
+            leads.append(lead)
+        panel = jnp.concatenate([panel_low, panel_high], axis=0)
         work[base : base + PANEL, :] = panel
         if base + PANEL < size:
+            start = base + PANEL
+            carried = []
+            for h in range(2):
+                rest = work[start + h * SUBS : start + (h + 1) * SUBS, :]
+                cols = [column(rest, base + j) for j in range(PANEL)]
+                for j in range(PANEL):
+                    lead_rest = cols[j] * scales[j]
+                    for m in range(j + 1, PANEL):
+                        cols[m] = cols[m] - lead_rest * leads[j][m]
+                    rest = rest - spread(lead_rest) * rows[j]
+                carried.append(rest)
+        if base + 2 * PANEL < size:
+            start = base + 2 * PANEL
             high, mid, low = three_parts(panel)
             first = jnp.concatenate([high, high, mid, high, low, mid], axis=0)[:, :size]
             second = jnp.concatenate([high, mid, high, low, high, mid], axis=0)
             update = narrow(first.astype(jnp.bfloat16), second.astype(jnp.bfloat16), ((0,), (0,)))
-            work[base + PANEL :, :] = work[base + PANEL :, :] - update[base + PANEL :, :]
-
-
-def bases_kernel(sweeps, gram_ref, start_ref, left_ref, right_ref, mass_ref, both, block, work):
+            work[start:, :] = work[start:, :] - update[start:, :]
+
+
+def pair(value):
+    return jnp.concatenate(two_parts(value), axis=1)
+
+
+def fold(wide, size):
+    return wide[:, :size] + wide[:, size:]
+
+
+def apply_parts(high, low, block):
+    size = block.shape[1]
+    parts = pair(block)
+    return fold(narrow(high, parts) + narrow(low, parts), size)
+
+
+def gram_parts(parts):
+    size = parts.shape[1] // 2
+    full = narrow(parts, parts, ((0,), (0,)))
+    return (full[:size, :size] + full[size:, size:]) + (full[:size, size:] + full[size:, :size])
+
+
+def right_apply(parts, factor):
+    turned = pair(factor.T)
+    return fold(narrow(parts, jnp.concatenate([turned, turned], axis=0)), factor.shape[0])
+
+
+def bases_kernel(sweeps, gram_ref, start_ref, left_ref, right_ref, mass_ref, both_high, both_low, block, work):
     rank, size = start_ref.shape
     for c in range(rank // LANES):
         cols = slice(c * LANES, (c + 1) * LANES)
         tile = gram_ref[c * rank : (c + 1) * rank, :]
-        both[1, :, cols] = tile
-        both[0, cols, :] = tile.T
+        high, low = two_parts(tile)
+        both_high[1, :, cols] = high
+        both_low[1, :, cols] = low
+        high, low = two_parts(tile.T)
+        both_high[0, cols, :] = high
+        both_low[0, cols, :] = low
     block[...] = start_ref[...]
     row = lax.broadcasted_iota(jnp.int32, (size, size), 0)
     col = lax.broadcasted_iota(jnp.int32, (size, size), 1)
     eye = (row == col).astype(jnp.float32)
 
     def step(k, carry):
-        product = exact(both[lax.rem(k, 2)], block[...])
-        work[:, :size] = exact(product, product, ((0,), (0,)))
+        turn = lax.rem(k, 2)
+        parts = pair(apply_parts(both_high[turn], both_low[turn], block[...]))
+        work[:, :size] = gram_parts(parts)
         work[:, size:] = eye
         inverse_factor(work, size)
         right_ref[...] = left_ref[...]
-        basis = exact(product, work[:, size:], ((1,), (1,)))
+        basis = right_apply(parts, work[:, size:])
         block[...] = basis
         left_ref[...] = basis
         return carry
 
     left_ref[...] = start_ref[...]
     lax.fori_loop(0, 2 * sweeps, step, 0)
-    mass_ref[...] = exact(left_ref[...], exact(both[1], right_ref[...]), ((0,), (0,)))
+    image = apply_parts(both_high[1], both_low[1], right_ref[...])
+    mass_ref[...] = exact(left_ref[...], image, ((0,), (0,)))
 
 
 def subspace_bases(cross_gram, start_block):
@@ -343,7 +404,8 @@
         in_specs=[vmem, vmem],
         out_specs=(vmem, vmem, vmem),
         scratch_shapes=[
-            pltpu.VMEM((2, rank, rank), jnp.float32),
+            pltpu.VMEM((2, rank, rank), jnp.bfloat16),
+            pltpu.VMEM((2, rank, rank), jnp.bfloat16),
             pltpu.VMEM((rank, size), jnp.float32),
             pltpu.VMEM((size, 2 * size), jnp.float32),
         ],

time: 156 us -> 140 us (0.90)
  Pallas kernels: 139 us -> 123 us
    pallas_call x1, Pallas kernels: 35 us -> 18.9 us  [subspace_bases(): pl.pallas_call(functools.partial(bases_kernel, 2), out_shape=(tall_shape,...]
where the time goes in v1:
time: 140 us; the launch traced here: 139 us
  Pallas kernels  123 us (88%)
  other arithmetic  10.9 us (8%)
  matrix products  3.13 us (2%)
  between operations  1.41 us (1%)
    pallas_call x1, Pallas kernels, all_reduce(): pl.pallas_call(functools.partial(all_reduce_kernel, nslab, nsub), out_sha...  37.6 us
    pallas_call x1, Pallas kernels, project(): pl.pallas_call(functools.partial(project_kernel, nslab, nsub, per_plane),...  33.1 us
    pallas_call x1, Pallas kernels, small_all_reduce(): pl.pallas_call(functools.partial(small_kernel, nslab, nsub), out_shape=ja...  20.7 us
    pallas_call x1, Pallas kernels, subspace_bases(): pl.pallas_call(functools.partial(bases_kernel, 2), out_shape=(tall_shape,...  18.9 us
    pallas_call x1, Pallas kernels, gram(): pl.pallas_call(gram_kernel, grid=(cells // step,), out_shape=jax.ShapeDty...  12.7 us
    div x1, other arithmetic, on_device(): conduct[..., None] * (beside - 6.0 * ctrl) / 6.0  7.25 us
    dot_general x3, matrix products, tall(): lax.dot_general(first, second, (dims, ((), ())), precision=HIGH, preferre...  3.13 us

profile of v1, /device:TPU:0, one launch (start us, length us, event | category | flops | bytes accessed | tf_op | source)
XLA Modules:
  0.0 139.0 jit_solution(17005168067152249253)
XLA Ops:
  0.6 12.7 %shard_map.102.in_ref = f32[512,512]{1,0:T(8,128)} custom-call(f32[4096,512]{1,0:T(8,128)} %bitcast.32, f32[4096,512]{1,0:T(8,128)} %bitcast.30), custom_call_target="tpu_custom_call" | custom-call | tf_op jit(solution)/shard_map/pallas_call | solution.py:64
  13.4 37.6 %shard_map.103.gram_ref = f32[2048,128]{1,0:T(8,128)} custom-call(f32[512,512]{1,0:T(8,128)} %shard_map.102.in_ref), custom_call_target="tpu_custom_call" | custom-call | tf_op jit(solution)/shard_map/pallas_call | solution.py:175
  50.9 18.9 %shard_map.104 = (f32[512,128]{1,0:T(8,128)}, f32[512,128]{1,0:T(8,128)}, f32[128,128]{1,0:T(8,128)}) custom-call(f32[2048,128]{1,0:T(8,128)} %shard_map.103.gram_ref, f32[512,128]{1,0:T(8,128)} %start_ref.1), custom_call_target="tpu_custom_call" | custom-call | tf_op jit(solution)/shard_map/pallas_call | solution.py:401
  69.9 33.1 %shard_map.105 = (f32[4,16,64,128]{3,2,1,0:T(8,128)}, f32[4096,128]{1,0:T(8,128)}, f32[16,64,128]{2,1,0:T(8,128)}, f32[16,64,128]{2,1,0:T(8,128)}, f32[4,64,128]{2,1,0:T(8,128)}, /*index=5*/f32[4,64,128]{2,1,0:T(8,128)}) custom-call(f32[4096,512]{1,0:T(8,128)} %bitcast.31, f32[4096,512]{1,0:T(8,128)} %bitcast.33, f32[512,128]{1,0:T(8,128)} %get-tuple-element.14.refs_2_, ...), custom_call_target="tpu_custom_call" | custom-call | tf_op jit(solution)/shard_map/pallas_call | solution.py:519
  103.0 0.0 copy-done.5
  103.1 0.1 mul.53
  103.1 7.2 %fusion.4 = f32[4,16,64,128]{3,2,1,0:T(8,128)S(1)} fusion(f32[4,16,64,128]{3,2,1,0:T(8,128)} %get-tuple-element.17, f32[4,1,64,128]{3,2,1,0:T(8,128)} %bitcast.40, f32[4,1,64,128]{3,2,1,0:T(8,128)} %bitcast.41, f32[1,16,64,128]{3,2,1,0:T(8,128)} %bitcast.36, f32[1,16,64,128]{3,2,1,0:T(8,128)} %bitcast.37, f32[4,16,64]{2,1,0:T(8,128)S(1)} %mul.53), kind=kLoop, calls=%fused_computation.6 | loop fusion | flops 6815744 | bytes 5521408 | tf_op jit(solution)/shard_map/div | solution.py:576
  110.4 0.0 copy-done
  110.4 0.0 copy-start.2
  110.4 0.0 copy-start.1
  110.4 1.9 %fusion.8 = f32[128,128]{1,0:T(8,128)S(1)} fusion(f32[4096,128]{1,0:T(8,128)S(1)} %copy-done, f32[4096,128]{1,0:T(8,128)S(1)} %bitcast.35), kind=kOutput, calls=%fused_computation.22 | convolution fusion | flops 402653184 | bytes 4259840 | tf_op jit(solution)/shard_map/dot_general | solution.py:23
  112.4 0.0 copy-start.3
  112.4 0.0 copy-done.2
  112.4 0.0 copy-done.1
  112.4 0.0 copy-start.4
  112.5 0.6 convolution_bitcast_fusion
  113.1 0.1 copy-done.3
  113.2 0.6 convolution_bitcast_fusion.1
  113.9 0.1 pad.8.clone
  113.9 0.7 maximum_maximum_fusion.in_ref
  114.7 20.7 %shard_map.106 = f32[192,128]{1,0:T(8,128)} custom-call(f32[192,128]{1,0:T(8,128)} %maximum_maximum_fusion.in_ref), custom_call_target="tpu_custom_call" | custom-call | tf_op jit(solution)/shard_map/pallas_call | solution.py:257
  136.0 0.0 copy-done.4
  136.1 1.6 %multiply_multiply_fusion = (f32[128,128]{1,0:T(8,128)}, f32[128,128]{1,0:T(8,128)}) fusion(f32[192,128]{1,0:T(8,128)} %shard_map.106, f32[128]{0:T(128)S(1)} %compare_convert_fusion, f32[128,128]{1,0:T(8,128)S(1)} %copy-done.4), kind=kLoop, calls=%fused_computation.17 | loop fusion | flops 49152 | bytes 263168 | tf_op jit(solution)/shard_map/mul | solution.py:594
  137.6 1.3 slice_multiply_fusion
  (6 shorter events, 0.1 us)
Async XLA Ops:
  69.9 33.2 %copy-start.5 = (f32[4,1024]{1,0:T(4,128)S(1)}, f32[4,1024]{1,0:T(4,128)}, u32[]{:S(2)}) copy-start(f32[4,1024]{1,0:T(4,128)} %param.9) | copy-start | bytes 49156
  103.1 7.3 %copy-start = (f32[4096,128]{1,0:T(8,128)S(1)}, f32[4096,128]{1,0:T(8,128)}, u32[]{:S(2)}) copy-start(f32[4096,128]{1,0:T(8,128)} %get-tuple-element.16) | copy-start | bytes 6291460
  110.4 2.0 %copy-start.2 = (f32[4,4,1024]{2,1,0:T(4,128)S(1)}, f32[4,4,1024]{2,1,0:T(4,128)}, u32[]{:S(2)}) copy-start(f32[4,4,1024]{2,1,0:T(4,128)} %param.11) | copy-start | bytes 196612
  110.4 2.0 %copy-start.1 = (f32[4,16,64,128]{3,2,1,0:T(8,128)S(1)}, f32[4,16,64,128]{3,2,1,0:T(8,128)}, u32[]{:S(2)}) copy-start(f32[4,16,64,128]{3,2,1,0:T(8,128)} %get-tuple-element.17) | copy-start | bytes 6291460
  112.4 0.8 copy-start.3
  112.4 23.6 %copy-start.4 = (f32[128,128]{1,0:T(8,128)S(1)}, f32[128,128]{1,0:T(8,128)}, u32[]{:S(2)}) copy-start(f32[128,128]{1,0:T(8,128)} %get-tuple-element.13) | copy-start | bytes 196612

commit v2 on v1

v2 whole, which is shorter than its diff:
```python
import functools
import jax
import jax.numpy as jnp
from jax import lax
from jax.experimental import pallas as pl
from jax.experimental.pallas import tpu as pltpu
from jax.sharding import PartitionSpec as P

LANES = 128
SUBS = 8
PANEL = 16
VMEM_BYTES = 60 * 1024 * 1024
HIGHEST = lax.Precision.HIGHEST


def exact(first, second, dims=((1,), (0,))):
    return lax.dot_general(
        first, second, (dims, ((), ())), precision=HIGHEST, preferred_element_type=jnp.float32
    )


def narrow(first, second, dims=((1,), (0,))):
    return lax.dot_general(first, second, (dims, ((), ())), preferred_element_type=jnp.float32)


def three_parts(value):
    high = value.astype(jnp.bfloat16).astype(jnp.float32)
    mid = (value - high).astype(jnp.bfloat16).astype(jnp.float32)
    return high, mid, value - high - mid


def two_parts(value):
    high = value.astype(jnp.bfloat16)
    return high, (value - high.astype(jnp.float32)).astype(jnp.bfloat16)


def three_dots(first, second, dims=((1,), (0,))):
    (a, b), (c, d) = two_parts(first), two_parts(second)
    return narrow(a, c, dims) + (narrow(a, d, dims) + narrow(b, c, dims))


def sub_bits(count):
    return [1 << b for b in range(count.bit_length() - 1)]


def across(block, sub):
    return jnp.broadcast_to(block[sub : sub + 1, :], block.shape)

def column(rows, lane):
    return jnp.broadcast_to(rows[:, lane : lane + 1], (SUBS, LANES))

def inverse_factor(work, size):
    wide = 2 * size // LANES
    place = lax.broadcasted_iota(jnp.int32, (SUBS, 2 * size), 0)
    spread = lambda x: jnp.concatenate([x] * wide, axis=1)
    carried = [work[h * SUBS : (h + 1) * SUBS, :] for h in range(2)]
    for base in range(0, size, PANEL):
        low, high = carried
        cols_low = [column(low, base + j) for j in range(SUBS)]
        cols_high = [column(high, base + j) for j in range(PANEL)]
        panel_low, panel_high = low, high
        scales, rows, leads = [], [], []
        for j in range(PANEL):
            if j < SUBS:
                scale = lax.rsqrt(across(cols_low[j], j))
                lead_low = cols_low[j] * scale
                row = across(low, j) * spread(scale)
                panel_low = jnp.where(place == j, row, panel_low)
            else:
                scale = lax.rsqrt(across(cols_high[j], j - SUBS))
                row = across(high, j - SUBS) * spread(scale)
                panel_high = jnp.where(place == j - SUBS, row, panel_high)
            lead_high = cols_high[j] * scale
            lead = {}
            for m in range(j + 1, PANEL):
                if m < SUBS:
                    lead[m] = across(lead_low, m)
                    cols_low[m] = cols_low[m] - lead_low * lead[m]
                else:
                    lead[m] = across(lead_high, m - SUBS)
                cols_high[m] = cols_high[m] - lead_high * lead[m]
            if j < SUBS - 1:
                low = low - spread(lead_low) * row
            if j < PANEL - 1:
                high = high - spread(lead_high) * row
            scales.append(scale)
            rows.append(row)
            leads.append(lead)
        panel = jnp.concatenate([panel_low, panel_high], axis=0)
        work[base : base + PANEL, :] = panel
        if base + PANEL < size:
            start = base + PANEL
            carried = []
            for h in range(2):
                rest = work[start + h * SUBS : start + (h + 1) * SUBS, :]
                cols = [column(rest, base + j) for j in range(PANEL)]
                for j in range(PANEL):
                    lead_rest = cols[j] * scales[j]
                    for m in range(j + 1, PANEL):
                        cols[m] = cols[m] - lead_rest * leads[j][m]
                    rest = rest - spread(lead_rest) * rows[j]
                carried.append(rest)
        if base + 2 * PANEL < size:
            start = base + 2 * PANEL
            high, mid, low = three_parts(panel)
            first = jnp.concatenate([high, high, mid, high, low, mid], axis=0)[:, :size]
            second = jnp.concatenate([high, mid, high, low, high, mid], axis=0)
            update = narrow(first.astype(jnp.bfloat16), second.astype(jnp.bfloat16), ((0,), (0,)))
            work[start:, :] = work[start:, :] - update[start:, :]


def pair(value):
    return jnp.concatenate(two_parts(value), axis=1)


def fold(wide, size):
    return wide[:, :size] + wide[:, size:]


def apply_parts(high, low, block):
    size = block.shape[1]
    parts = pair(block)
    return fold(narrow(high, parts) + narrow(low, parts), size)


def gram_parts(parts):
    size = parts.shape[1] // 2
    full = narrow(parts, parts, ((0,), (0,)))
    return (full[:size, :size] + full[size:, size:]) + (full[:size, size:] + full[size:, :size])


def right_apply(parts, factor):
    turned = pair(factor.T)
    return fold(narrow(parts, jnp.concatenate([turned, turned], axis=0)), factor.shape[0])


def far_count(nslab):
    return max(nslab // 2, 1)


def front_kernel(nslab, nsub, points, *refs):
    obs_hbm, ctrl_hbm, conduct_ref, drive_ref, sense_ref = refs[:5]
    gram_ref, inner_ref, maps_ref = refs[5:8]
    obs, ctrl, spread_k, applied_high, applied_low, acc, work, got, got_far, load = refs[8:18]
    rs_send, rs_recv, far_send, far_recv, back_send, back_recv, ag_send, ag_recv = refs[18:]
    slab, sub = lax.axis_index("slab"), lax.axis_index("sub")
    cells, wide = ctrl.shape
    planes, plane_cells = conduct_ref.shape
    step = applied_high.shape[0]
    count = cells // step
    nfar = far_count(nslab)
    turns = [("sub", bit) for bit in sub_bits(nsub)] + [("slab", 1)]
    orders = (turns, turns[:1] + turns[1:][::-1])

    def fetch(which, k):
        rows = pl.ds(k * step, step)
        source, target = ((obs_hbm, obs), (ctrl_hbm, ctrl))[which]
        return pltpu.make_async_copy(source.at[rows], target.at[rows], load.at[which, k])

    for k in range(count):
        fetch(0, k).start()
        fetch(1, k).start()

    def partner(axis, bit):
        index = slab if axis == "slab" else sub
        has = lax.rem(index // bit, 2)
        return has, {axis: index + bit - 2 * bit * has}

    def far(off):
        other = lax.rem(slab // 2 + off, nfar)
        return other, {"slab": other * 2 + lax.rem(slab, 2)}

    barrier = pltpu.get_barrier_semaphore()
    for axis, bit in turns:
        pl.semaphore_signal(barrier, inc=1, device_id=partner(axis, bit)[1])
    for off in range(1, nfar):
        pl.semaphore_signal(barrier, inc=1, device_id=far(off)[1])

    for p in range(planes):
        for c in range(plane_cells // LANES):
            lanes = conduct_ref[p : p + 1, c * LANES : (c + 1) * LANES] * (1.0 / 6.0)
            first = p * plane_cells + c * LANES
            spread_k[first : first + LANES, :] = jnp.broadcast_to(lanes, (LANES, LANES)).T
    acc[...] = jnp.zeros_like(acc)

    def add_block(k, carry):
        fetch(0, k).wait()
        fetch(1, k).wait()
        rows = pl.ds(pl.multiple_of(k * step, step), step)
        acc[...] += three_dots(obs[rows, :], ctrl[rows, :], ((0,), (0,)))
        return carry

    lax.fori_loop(0, count, add_block, 0)
    tall_rows = acc.shape[0]
    for c in range(acc.shape[1] // LANES):
        work[c * tall_rows : (c + 1) * tall_rows, :] = acc[:, c * LANES : (c + 1) * LANES]
    pl.semaphore_wait(barrier, len(turns) + nfar - 1)

    place = lax.broadcasted_iota(jnp.int32, (points, wide), 0)

    def inner_block(k):
        first = k * step
        plane = first // plane_cells

        def line(i, carry):
            row = pl.multiple_of(first + i * points, points)
            within = lax.rem(row, plane_cells)
            here = ctrl[pl.ds(row, points), :]
            total = jnp.where(place > 0, pltpu.roll(here, 1, 0), 0.0)
            total = total + jnp.where(place < points - 1, pltpu.roll(here, points - 1, 0), 0.0)
            before = pl.multiple_of(jnp.maximum(row - points, 0), points)
            after = pl.multiple_of(jnp.minimum(row + points, cells - points), points)
            total = total + jnp.where(within > 0, 1.0, 0.0) * ctrl[pl.ds(before, points), :]
            inside = jnp.where(within < plane_cells - points, 1.0, 0.0)
            total = total + inside * ctrl[pl.ds(after, points), :]
            if plane > 0:
                total = total + ctrl[pl.ds(row - plane_cells, points), :]
            if plane < planes - 1:
                total = total + ctrl[pl.ds(row + plane_cells, points), :]
            scale = jnp.concatenate([spread_k[pl.ds(row, points), :]] * (wide // LANES), axis=1)
            high, low = two_parts(scale * (total - 6.0 * here))
            applied_high[pl.ds(pl.multiple_of(i * points, points), points), :] = high
            applied_low[pl.ds(pl.multiple_of(i * points, points), points), :] = low
            return carry

        lax.fori_loop(0, step // points, line, 0)
        rows = slice(first, first + step)
        high, low = two_parts(obs[rows, :])
        dims = ((0,), (0,))
        value = narrow(high, applied_high[...], dims) + (
            narrow(high, applied_low[...], dims) + narrow(low, applied_high[...], dims)
        )
        lanes = slice(first % plane_cells, first % plane_cells + step)
        seen = three_dots(drive_ref[:, plane, lanes], obs[rows, :])
        felt = three_dots(sense_ref[:, plane, lanes], ctrl[rows, :])
        both = jnp.concatenate([seen, felt], axis=0)
        if k == 0:
            inner_ref[...] = value
            maps_ref[...] = both
        else:
            inner_ref[...] += value
            maps_ref[...] += both

    blocks = iter(range(count))

    def work_meanwhile(amount):
        for _ in range(amount):
            k = next(blocks, None)
            if k is not None:
                inner_block(k)

    gaps = 2 * len(turns) + 2
    share = -(-count // gaps)
    rows = work.shape[0]
    length = rows // 2
    bases, taken = [0, length], 0
    for s in range(len(turns)):
        length = length // 2
        copies, keeps = [], []
        for h in range(2):
            axis, bit = orders[h][s]
            has, target = partner(axis, bit)
            keeps.append(pl.multiple_of(bases[h] + has * length, 8))
            give = pl.multiple_of(bases[h] + (1 - has) * length, 8)
            copies.append(
                pltpu.make_async_remote_copy(
                    src_ref=work.at[pl.ds(give, length)],
                    dst_ref=got.at[h, pl.ds(taken, length)],
                    send_sem=rs_send.at[h, s],
                    recv_sem=rs_recv.at[h, s],
                    device_id=target,
                )
            )
            copies[h].start()
        work_meanwhile(share)
        for h in range(2):
            copies[h].wait()
            work[pl.ds(keeps[h], length), :] += got[h, taken : taken + length, :]
        bases, taken = keeps, taken + length

    piece = length // nfar
    mines = [pl.multiple_of(bases[h] + (slab // 2) * piece, 8) for h in range(2)]
    copies = []
    for h in range(2):
        for off in range(1, nfar):
            other, target = far(off)
            copy = pltpu.make_async_remote_copy(
                src_ref=work.at[pl.ds(pl.multiple_of(bases[h] + other * piece, 8), piece)],
                dst_ref=got_far.at[h, off],
                send_sem=far_send.at[h, off],
                recv_sem=far_recv.at[h, off],
                device_id=target,
            )
            copy.start()
            copies.append(copy)
    work_meanwhile(share)
    for copy in copies:
        copy.wait()
    for h in range(2):
        total = work[pl.ds(mines[h], piece), :]
        for off in range(1, nfar):
            total = total + got_far[h, off]
        gram_ref[pl.ds(mines[h], piece), :] = total

    copies = []
    for h in range(2):
        for off in range(1, nfar):
            copy = pltpu.make_async_remote_copy(
                src_ref=gram_ref.at[pl.ds(mines[h], piece)],
                dst_ref=gram_ref.at[pl.ds(mines[h], piece)],
                send_sem=back_send.at[h, off],
                recv_sem=back_recv.at[h, off],
                device_id=far(off)[1],
            )
            copy.start()
            copies.append(copy)
    work_meanwhile(share)
    for copy in copies:
        copy.wait()

    for s in reversed(range(len(turns))):
        copies, nexts = [], []
        for h in range(2):
            axis, bit = orders[h][s]
            has, target = partner(axis, bit)
            copy = pltpu.make_async_remote_copy(
                src_ref=gram_ref.at[pl.ds(bases[h], length)],
                dst_ref=gram_ref.at[pl.ds(bases[h], length)],
                send_sem=ag_send.at[h, s],
                recv_sem=ag_recv.at[h, s],
                device_id=target,
            )
            copy.start()
            copies.append(copy)
            nexts.append(pl.multiple_of(bases[h] - has * length, 8))
        work_meanwhile(share if s else count)
        for copy in copies:
            copy.wait()
        bases, length = nexts, 2 * length


def front(factor_obs, factor_ctrl, diffusivity, input_map, output_map, ident):
    nslab, nsub = lax.axis_size("slab"), lax.axis_size("sub")
    planes, lines, points, wide = factor_ctrl.shape
    cells = planes * lines * points
    step = lines * points // (2 if lines % 2 == 0 else 1)
    rows = wide * (wide // LANES)
    nfar, turns = far_count(nslab), len(sub_bits(nsub)) + 1
    half = rows // 2
    maps = input_map.shape[0] + output_map.shape[0]
    vmem, anywhere = pl.BlockSpec(memory_space=pltpu.VMEM), pl.BlockSpec(memory_space=pl.ANY)
    near, far = pltpu.SemaphoreType.DMA((2, turns)), pltpu.SemaphoreType.DMA((2, nfar))
    f32, bf16 = jnp.float32, jnp.bfloat16
    return pl.pallas_call(
        functools.partial(front_kernel, nslab, nsub, points),
        out_shape=[
            jax.ShapeDtypeStruct((rows, LANES), f32),
            jax.ShapeDtypeStruct((wide, wide), f32),
            jax.ShapeDtypeStruct((maps, wide), f32),
        ],
        in_specs=[anywhere, anywhere, vmem, vmem, vmem],
        out_specs=[vmem, vmem, vmem],
        scratch_shapes=[
            pltpu.VMEM((cells, wide), f32),
            pltpu.VMEM((cells, wide), f32),
            pltpu.VMEM((cells, LANES), f32),
            pltpu.VMEM((step, wide), bf16),
            pltpu.VMEM((step, wide), bf16),
            pltpu.VMEM((wide, wide), f32),
            pltpu.VMEM((rows, LANES), f32),
            pltpu.VMEM((2, half, LANES), f32),
            pltpu.VMEM((2, nfar, half // 2**turns // nfar, LANES), f32),
            pltpu.SemaphoreType.DMA((2, cells // step)),
            near, near, far, far, far, far, near, near,
        ],
        compiler_params=pltpu.CompilerParams(
            collective_id=ident, has_side_effects=True, vmem_limit_bytes=VMEM_BYTES
        ),
    )(
        factor_obs.reshape(cells, wide),
        factor_ctrl.reshape(cells, wide),
        diffusivity,
        input_map,
        output_map,
    )


def face_chunks(cells):
    return 2 if cells % 16 == 0 else 1


def back_kernel(nslab, nsub, points, sweeps, *refs):
    order_ref, gram_ref, start_ref, inner_ref, maps_ref, conduct_ref, obs_hbm, ctrl_hbm = refs[:8]
    mass_ref, state_ref, in_ref, out_ref = refs[8:12]
    both_high, both_low, block, left_ref, right_ref, work, turned, face = refs[12:20]
    obs_z, obs_y, ctrl_z, ctrl_y, send_z, send_y, got_z, got_y = refs[20:28]
    flat, pack, slots, result = refs[28:32]
    load, z_send, z_recv, y_send, y_recv, rs_send, rs_recv, ag_send, ag_recv = refs[32:]
    slab, sub = lax.axis_index("slab"), lax.axis_index("sub")
    rank, size = start_ref.shape
    planes, plane_cells = conduct_ref.shape
    total, me = nslab * nsub, slab * nsub + sub
    chunks = face_chunks(plane_cells)
    chunk = plane_cells // chunks

    def peer(off):
        other = lax.rem(me + off, total)
        return other, {"slab": other // nsub, "sub": lax.rem(other, nsub)}

    barrier = pltpu.get_barrier_semaphore()

    def greet(off, carry):
        pl.semaphore_signal(barrier, inc=1, device_id=peer(off)[1])
        return carry

    lax.fori_loop(1, total, greet, 0)

    loads = []
    for which, (source, z_face, y_face) in enumerate(
        ((ctrl_hbm, ctrl_z, ctrl_y), (obs_hbm, obs_z, obs_y))
    ):
        for side in range(2):
            plane = side * (planes - 1)
            pairs = [(source.at[pl.ds(plane * plane_cells, plane_cells)], z_face.at[side])]
            for p in range(planes):
                first = p * plane_cells + side * (plane_cells - points)
                pairs.append(
                    (source.at[pl.ds(first, points)], y_face.at[side, pl.ds(p * points, points)])
                )
            for i, (here, there) in enumerate(pairs):
                loads.append(pltpu.make_async_copy(here, there, load.at[which, side, i]))
    for copy in loads:
        copy.start()

    for c in range(rank // LANES):
        cols = slice(c * LANES, (c + 1) * LANES)
        tile = gram_ref[c * rank : (c + 1) * rank, :]
        high, low = two_parts(tile)
        both_high[1, :, cols] = high
        both_low[1, :, cols] = low
        high, low = two_parts(tile.T)
        both_high[0, cols, :] = high
        both_low[0, cols, :] = low
    block[...] = start_ref[...]
    row = lax.broadcasted_iota(jnp.int32, (size, size), 0)
    col = lax.broadcasted_iota(jnp.int32, (size, size), 1)
    eye = (row == col).astype(jnp.float32)
    pl.semaphore_wait(barrier, total - 1)

    places = (("slab", slab, nslab, 1), ("slab", slab, nslab, -1))
    places = places + (("sub", sub, nsub, 1), ("sub", sub, nsub, -1))

    def beside(m, way):
        _, index, count, step = places[m]
        return index < count - 1 if step * way > 0 else index > 0

    def copy_z(m, c):
        axis, index, _, step = places[m]
        return pltpu.make_async_remote_copy(
            src_ref=send_z.at[m, c],
            dst_ref=got_z.at[m, c],
            send_sem=z_send.at[m, c],
            recv_sem=z_recv.at[m, c],
            device_id={axis: index + step},
        )

    def copy_y(m):
        axis, index, _, step = places[2 + m]
        return pltpu.make_async_remote_copy(
            src_ref=send_y.at[m],
            dst_ref=got_y.at[m],
            send_sem=y_send.at[m],
            recv_sem=y_recv.at[m],
            device_id={axis: index + step},
        )

    def project(cells, parts):
        high, low = two_parts(cells)
        return fold(narrow(high, parts) + narrow(low, parts), size)

    def send_faces():
        parts = pair(apply_parts(both_high[1], both_low[1], block[...]))
        image = narrow(both_high[0], parts) + narrow(both_low[0], parts)
        parts = pair(fold(image, size))
        for copy in loads[: len(loads) // 2]:
            copy.wait()
        for c in range(chunks):
            for m in range(2):
                rows = slice(c * chunk, (c + 1) * chunk)
                send_z[m, c] = project(ctrl_z[1 - m, rows, :], parts)

                @pl.when(beside(m, 1))
                def _():
                    copy_z(m, c).start()

        for m in range(2):
            send_y[m] = project(ctrl_y[1 - m], parts)

            @pl.when(beside(2 + m, 1))
            def _():
                copy_y(m).start()

    def step(k, carry):
        turn = lax.rem(k, 2)
        parts = pair(apply_parts(both_high[turn], both_low[turn], block[...]))
        work[:, :size] = gram_parts(parts)
        work[:, size:] = eye
        inverse_factor(work, size)
        right_ref[...] = left_ref[...]
        basis = right_apply(parts, work[:, size:])
        block[...] = basis
        left_ref[...] = basis

        @pl.when(k == 2 * sweeps - 4)
        def _():
            send_faces()
            turned[...] = eye

        @pl.when(jnp.logical_and(k > 2 * sweeps - 4, k < 2 * sweeps - 1))
        def _():
            turned[...] = exact(turned[...], work[:, size:], ((1,), (1,)))

        return carry

    left_ref[...] = start_ref[...]
    lax.fori_loop(0, 2 * sweeps, step, 0)

    left_parts, right_parts = pair(left_ref[...]), pair(right_ref[...])
    image = fold(narrow(both_high[1], right_parts) + narrow(both_low[1], right_parts), size)
    kept = order_ref[0]
    square = jnp.where(jnp.logical_and(row < kept, col < kept), 1.0, 0.0)
    mass_ref[...] = square * exact(left_ref[...], image, ((0,), (0,)))
    state = exact(left_ref[...], project(inner_ref[...], right_parts), ((0,), (0,)))
    maps = maps_ref.shape[0]
    ins = in_ref.shape[1]
    seen = project(maps_ref[...], left_parts)
    felt = project(maps_ref[...], right_parts)
    side = lax.broadcasted_iota(jnp.int32, seen.shape, 0)
    flat[...] = jnp.zeros_like(flat)
    flat[size : size + maps, :] = jnp.where(side < ins, seen, felt)
    for copy in loads[len(loads) // 2 :]:
        copy.wait()

    def spread(plane, group):
        lanes = conduct_ref[plane : plane + 1, group * LANES : (group + 1) * LANES] * (1.0 / 6.0)
        return jnp.broadcast_to(lanes, (LANES, LANES)).T

    groups = plane_cells // LANES
    face[...] = jnp.zeros_like(face)
    for m in range(2):
        mine = project(obs_y[m], left_parts)
        last = [spread(p, m * (groups - 1)) for p in range(planes)]
        scale = [part[LANES - points :] if m else part[:points] for part in last]
        mine = mine * jnp.concatenate(scale, axis=0)

        @pl.when(beside(2 + m, -1))
        def _():
            copy_y(m).wait_recv()
            face[...] += three_dots(mine, got_y[m], ((0,), (0,)))

    for c in range(chunks):
        for m in range(2):
            rows = slice(c * chunk, (c + 1) * chunk)
            mine = project(obs_z[m, rows, :], left_parts)
            per = groups // chunks
            scale = [spread(m * (planes - 1), c * per + g) for g in range(per)]
            mine = mine * jnp.concatenate(scale, axis=0)

            @pl.when(beside(m, -1))
            def _():
                copy_z(m, c).wait_recv()
                face[...] += three_dots(mine, got_z[m, c], ((0,), (0,)))

    flat[:size, :] = state + exact(face[...], turned[...])
    part = pack.shape[1]
    owners = -(-(size + maps) // part)
    pack[...] = jnp.zeros_like(pack)
    for d in range(owners):
        pack[d] = flat[d * part : (d + 1) * part, :]

    def gather(off):
        other, target = peer(off)
        return pltpu.make_async_remote_copy(
            src_ref=pack.at[other],
            dst_ref=slots.at[off],
            send_sem=rs_send.at[off],
            recv_sem=rs_recv.at[off],
            device_id=target,
        )

    def spread_out(off):
        return pltpu.make_async_remote_copy(
            src_ref=result.at[me],
            dst_ref=result.at[me],
            send_sem=ag_send.at[off],
            recv_sem=ag_recv.at[off],
            device_id=peer(off)[1],
        )

    def loop(act):
        def body(off, carry):
            act(off)
            return carry

        lax.fori_loop(1, total, body, 0)

    loop(lambda off: gather(off).start())
    slots[0] = pack[me]
    loop(lambda off: gather(off).wait())
    result[me] = jnp.sum(slots[...], axis=0)
    loop(lambda off: spread_out(off).start())
    for m in range(2):

        @pl.when(beside(2 + m, 1))
        def _():
            copy_y(m).wait_send()

        for c in range(chunks):

            @pl.when(beside(m, 1))
            def _():
                copy_z(m, c).wait_send()

    loop(lambda off: spread_out(off).wait())
    for d in range(owners):
        flat[d * part : (d + 1) * part, :] = result[d]
    state_ref[...] = square * flat[:size, :]
    lanes = jnp.where(col[:maps, :] < kept, 1.0, 0.0) * flat[size : size + maps, :]
    in_ref[...] = lanes.T[:, :ins]
    out_ref[...] = lanes[ins:, :]


def back(order, gram, start, inner, maps, diffusivity, factor_obs, factor_ctrl, ins, ident):
    nslab, nsub = lax.axis_size("slab"), lax.axis_size("sub")
    planes, lines, points, wide = factor_ctrl.shape
    cells, plane_cells = planes * lines * points, lines * points
    rank, size = start.shape
    total = nslab * nsub
    rows = size + maps.shape[0]
    part = -(-rows // total)
    chunks = face_chunks(plane_cells)
    side = planes * points
    f32, bf16 = jnp.float32, jnp.bfloat16
    vmem, anywhere = pl.BlockSpec(memory_space=pltpu.VMEM), pl.BlockSpec(memory_space=pl.ANY)
    every = pltpu.SemaphoreType.DMA((total,))
    zs, ys = pltpu.SemaphoreType.DMA((2, chunks)), pltpu.SemaphoreType.DMA((2,))
    faces_z = pltpu.VMEM((2, chunks, plane_cells // chunks, size), f32)
    faces_y = pltpu.VMEM((2, side, size), f32)
    return pl.pallas_call(
        functools.partial(back_kernel, nslab, nsub, points, 2),
        out_shape=[
            jax.ShapeDtypeStruct((size, size), f32),
            jax.ShapeDtypeStruct((size, size), f32),
            jax.ShapeDtypeStruct((size, ins), f32),
            jax.ShapeDtypeStruct((maps.shape[0] - ins, size), f32),
        ],
        in_specs=[pl.BlockSpec(memory_space=pltpu.SMEM)] + [vmem] * 5 + [anywhere] * 2,
        out_specs=[vmem] * 4,
        scratch_shapes=[
            pltpu.VMEM((2, rank, rank), bf16),
            pltpu.VMEM((2, rank, rank), bf16),
            pltpu.VMEM((rank, size), f32),
            pltpu.VMEM((rank, size), f32),
            pltpu.VMEM((rank, size), f32),
            pltpu.VMEM((size, 2 * size), f32),
            pltpu.VMEM((size, size), f32),
            pltpu.VMEM((size, size), f32),
            pltpu.VMEM((2, plane_cells, wide), f32),
            pltpu.VMEM((2, side, wide), f32),
            pltpu.VMEM((2, plane_cells, wide), f32),
            pltpu.VMEM((2, side, wide), f32),
            faces_z, faces_y, faces_z, faces_y,
            pltpu.VMEM((part * -(-rows // part), LANES), f32),
            pltpu.VMEM((total, part, LANES), f32),
            pltpu.VMEM((total, part, LANES), f32),
            pltpu.VMEM((total, part, LANES), f32),
            pltpu.SemaphoreType.DMA((2, 2, planes + 1)),
            zs, zs, ys, ys, every, every, every, every,
        ],
        compiler_params=pltpu.CompilerParams(
            collective_id=ident, has_side_effects=True, vmem_limit_bytes=VMEM_BYTES
        ),
    )(
        order,
        gram,
        start,
        inner,
        maps,
        diffusivity,
        factor_obs.reshape(cells, wide),
        factor_ctrl.reshape(cells, wide),
    )


def on_device(factor_obs, factor_ctrl, diffusivity, input_map, output_map, start_block, order):
    gram, inner, maps = front(factor_obs, factor_ctrl, diffusivity, input_map, output_map, 0)
    ins = input_map.shape[0]
    return tuple(
        back(order, gram, start_block, inner, maps, diffusivity, factor_obs, factor_ctrl, ins, 1)
    )


def solution(mesh):
    placed = (
        P("slab", "sub", None, None),
        P("slab", "sub", None, None),
        P("slab", "sub"),
        P(None, "slab", "sub"),
        P(None, "slab", "sub"),
        P(),
        P(),
    )
    return jax.shard_map(
        on_device, mesh=mesh, in_specs=placed, out_specs=(P(), P(), P(), P()), check_vma=False
    )
```

time: 140 us -> 101 us (0.72)
  Pallas kernels: 123 us -> 93.7 us
  other arithmetic: 10.9 us -> 0 us
  local copies, waits for them, and re-layouts: 0.42 us -> 5.68 us
  matrix products: 3.13 us -> 0 us
    pallas_call x5 -> x2, Pallas kernels: 123 us -> 93.7 us  [the longest x1 49.1 us: back(): pl.pallas_call(functools.partial(back_kernel, nslab, nsub, points, 2), ou...]
    div x1 -> x0, other arithmetic: 7.25 us -> none  [on_device(): conduct[..., None] * (beside - 6.0 * ctrl) / 6.0]
    unnamed x14 -> x3, local copies, waits for them, and re-layouts: 0.26 us -> 4.19 us
    dot_general x3 -> x0, matrix products: 3.13 us -> none  [tall(): lax.dot_general(first, second, (dims, ((), ())), precision=HIGH, preferre...]
    mul x2 -> x0, other arithmetic: 2.92 us -> none  [the longest x1 1.58 us: on_device(): square * summed[:size]]
    pallas_call x0 -> x1, local copies, waits for them, and re-layouts: none -> 1.49 us  [back(): pl.pallas_call(functools.partial(back_kernel, nslab, nsub, points, 2), ou...]
where the time goes in v2:
time: 101 us
  Pallas kernels  93.7 us (93%)
  local copies, waits for them, and re-layouts  5.68 us (6%)
  between operations  1.3 us (1%)
    pallas_call x1, Pallas kernels, back(): pl.pallas_call(functools.partial(back_kernel, nslab, nsub, points, 2), ou...  49.1 us
    pallas_call x1, Pallas kernels, front(): pl.pallas_call(functools.partial(front_kernel, nslab, nsub, points), out_...  44.6 us
    unnamed x3, local copies, waits for them, and re-layouts  4.19 us

profile of v2, /device:TPU:0, one launch (start us, length us, event | category | flops | bytes accessed | tf_op | source)
XLA Modules:
  0.0 100.7 jit_solution(2966248609198078831)
XLA Ops:
  1.3 44.6 %shard_map.102 = (f32[2048,128]{1,0:T(8,128)}, f32[512,512]{1,0:T(8,128)}, f32[8,512]{1,0:T(8,128)}) custom-call(f32[4096,512]{1,0:T(8,128)} %bitcast.2, f32[4096,512]{1,0:T(8,128)} %bitcast.4, f32[4,1024]{1,0:T(4,128)} %refs_5_.1, f32[4,4,1024]{2,1,0:T(4,128)} %refs_3_.1, f32[4,4,1024]{2,1,0:T(4,128)} %refs_4_.1), custom_call_target="tpu_custom_call" | custom-call | tf_op jit(solution)/shard_map/pallas_call | solution.py:354
  45.9 49.1 %shard_map.103 = (f32[128,128]{1,0:T(8,128)}, f32[128,128]{1,0:T(8,128)}, f32[128,4]{1,0:T(8,128)}, f32[4,128]{1,0:T(4,128)}) custom-call(s32[1]{0:T(128)S(6)} %copy.15.refs_0_, f32[2048,128]{1,0:T(8,128)} %get-tuple-element.7.refs_1_, f32[512,128]{1,0:T(8,128)} %refs_2_.3, f32[512,512]{1,0:T(8,128)} %get-tuple-element.8.refs_3_, ...), custom_call_target="tpu_custom_call" | custom-call | tf_op jit(solution)/shard_map/pallas_call | solution.py:649
  95.0 1.5 %copy.11 = f32[128,4]{0,1:T(4,128)} copy(f32[128,4]{1,0:T(8,128)} %get-tuple-element.12) | data formatting | bytes 4096 | tf_op jit(solution)/shard_map/pallas_call | solution.py:649
  96.5 1.5 %copy.16 = f32[128,128]{1,0:T(8,128)} copy(f32[128,128]{1,0:T(8,128)} %get-tuple-element.18) | data formatting | bytes 131072
  98.0 1.5 %copy.17 = f32[128,128]{1,0:T(8,128)} copy(f32[128,128]{1,0:T(8,128)} %get-tuple-element.19) | data formatting | bytes 131072
  99.4 1.2 %copy.18 = f32[4,128]{1,0:T(4,128)} copy(f32[4,128]{1,0:T(4,128)} %get-tuple-element.21) | data formatting | bytes 4096

commit v3 on v2

--- a/solution.py
+++ b/solution.py
@@ -41,6 +41,14 @@
 
 def sub_bits(count):
     return [1 << b for b in range(count.bit_length() - 1)]
+
+
+def far_count(nslab):
+    return max(nslab // 2, 1)
+
+
+def face_chunks(cells):
+    return 2 if cells % 16 == 0 else 1
 
 
 def across(block, sub):
@@ -134,18 +142,29 @@
     return fold(narrow(parts, jnp.concatenate([turned, turned], axis=0)), factor.shape[0])
 
 
-def far_count(nslab):
-    return max(nslab // 2, 1)
-
-
-def front_kernel(nslab, nsub, points, *refs):
-    obs_hbm, ctrl_hbm, conduct_ref, drive_ref, sense_ref = refs[:5]
-    gram_ref, inner_ref, maps_ref = refs[5:8]
-    obs, ctrl, spread_k, applied_high, applied_low, acc, work, got, got_far, load = refs[8:18]
-    rs_send, rs_recv, far_send, far_recv, back_send, back_recv, ag_send, ag_recv = refs[18:]
+def peers(slab, sub, nslab, nsub):
+    everyone, me = nslab * nsub, slab * nsub + sub
+
+    def peer(off):
+        other = lax.rem(me + off, everyone)
+        return other, {"slab": other // nsub, "sub": lax.rem(other, nsub)}
+
+    return everyone, me, peer
+
+
+def whole_kernel(nslab, nsub, points, sweeps, *refs):
+    obs_hbm, ctrl_hbm, conduct_hbm, drive_hbm, sense_hbm, start_hbm, out_ref = refs[:7]
+    obs, ctrl, conduct, drive, sense, start, spread_k, applied_high, applied_low = refs[7:16]
+    acc, inner, maps, work, got, got_far, whole = refs[16:23]
+    both_high, both_low, left, right, square, turned, face = refs[23:30]
+    send_z, send_y, got_z, got_y, pack, slots, result = refs[30:37]
+    load, load_small = refs[37:39]
+    rs_send, rs_recv, far_send, far_recv, back_send, back_recv, ag_send, ag_recv = refs[39:47]
+    z_send, z_recv, y_send, y_recv, sum_send, sum_recv, give_send, give_recv = refs[47:]
     slab, sub = lax.axis_index("slab"), lax.axis_index("sub")
+    everyone, me, peer = peers(slab, sub, nslab, nsub)
     cells, wide = ctrl.shape
-    planes, plane_cells = conduct_ref.shape
+    planes, plane_cells = conduct.shape
     step = applied_high.shape[0]
     count = cells // step
     nfar = far_count(nslab)
@@ -157,9 +176,18 @@
         source, target = ((obs_hbm, obs), (ctrl_hbm, ctrl))[which]
         return pltpu.make_async_copy(source.at[rows], target.at[rows], load.at[which, k])
 
+    small = [
+        pltpu.make_async_copy(here, there, load_small.at[i])
+        for i, (here, there) in enumerate(
+            ((conduct_hbm, conduct), (drive_hbm, drive), (sense_hbm, sense), (start_hbm, start))
+        )
+    ]
+    small[0].start()
     for k in range(count):
         fetch(0, k).start()
         fetch(1, k).start()
+    for copy in small[1:]:
+        copy.start()
 
     def partner(axis, bit):
         index = slab if axis == "slab" else sub
@@ -171,14 +199,16 @@
         return other, {"slab": other * 2 + lax.rem(slab, 2)}
 
     barrier = pltpu.get_barrier_semaphore()
-    for axis, bit in turns:
-        pl.semaphore_signal(barrier, inc=1, device_id=partner(axis, bit)[1])
-    for off in range(1, nfar):
-        pl.semaphore_signal(barrier, inc=1, device_id=far(off)[1])
-
+
+    def greet(off, carry):
+        pl.semaphore_signal(barrier, inc=1, device_id=peer(off)[1])
+        return carry
+
+    lax.fori_loop(1, everyone, greet, 0)
+    small[0].wait()
     for p in range(planes):
         for c in range(plane_cells // LANES):
-            lanes = conduct_ref[p : p + 1, c * LANES : (c + 1) * LANES] * (1.0 / 6.0)
+            lanes = conduct[p : p + 1, c * LANES : (c + 1) * LANES] * (1.0 / 6.0)
             first = p * plane_cells + c * LANES
             spread_k[first : first + LANES, :] = jnp.broadcast_to(lanes, (LANES, LANES)).T
     acc[...] = jnp.zeros_like(acc)
@@ -194,7 +224,9 @@
     tall_rows = acc.shape[0]
     for c in range(acc.shape[1] // LANES):
         work[c * tall_rows : (c + 1) * tall_rows, :] = acc[:, c * LANES : (c + 1) * LANES]
-    pl.semaphore_wait(barrier, len(turns) + nfar - 1)
+    for copy in small[1:]:
+        copy.wait()
+    pl.semaphore_wait(barrier, everyone - 1)
 
     place = lax.broadcasted_iota(jnp.int32, (points, wide), 0)
 
@@ -231,15 +263,15 @@
             narrow(high, applied_low[...], dims) + narrow(low, applied_high[...], dims)
         )
         lanes = slice(first % plane_cells, first % plane_cells + step)
-        seen = three_dots(drive_ref[:, plane, lanes], obs[rows, :])
-        felt = three_dots(sense_ref[:, plane, lanes], ctrl[rows, :])
+        seen = three_dots(drive[:, plane, lanes], obs[rows, :])
+        felt = three_dots(sense[:, plane, lanes], ctrl[rows, :])
         both = jnp.concatenate([seen, felt], axis=0)
         if k == 0:
-            inner_ref[...] = value
-            maps_ref[...] = both
+            inner[...] = value
+            maps[...] = both
         else:
-            inner_ref[...] += value
-            maps_ref[...] += both
+            inner[...] += value
+            maps[...] += both
 
     blocks = iter(range(count))
 
@@ -300,14 +332,14 @@
         total = work[pl.ds(mines[h], piece), :]
         for off in range(1, nfar):
             total = total + got_far[h, off]
-        gram_ref[pl.ds(mines[h], piece), :] = total
+        whole[pl.ds(mines[h], piece), :] = total
 
     copies = []
     for h in range(2):
         for off in range(1, nfar):
             copy = pltpu.make_async_remote_copy(
-                src_ref=gram_ref.at[pl.ds(mines[h], piece)],
-                dst_ref=gram_ref.at[pl.ds(mines[h], piece)],
+                src_ref=whole.at[pl.ds(mines[h], piece)],
+                dst_ref=whole.at[pl.ds(mines[h], piece)],
                 send_sem=back_send.at[h, off],
                 recv_sem=back_recv.at[h, off],
                 device_id=far(off)[1],
@@ -324,8 +356,8 @@
             axis, bit = orders[h][s]
             has, target = partner(axis, bit)
             copy = pltpu.make_async_remote_copy(
-                src_ref=gram_ref.at[pl.ds(bases[h], length)],
-                dst_ref=gram_ref.at[pl.ds(bases[h], length)],
+                src_ref=whole.at[pl.ds(bases[h], length)],
+                dst_ref=whole.at[pl.ds(bases[h], length)],
                 send_sem=ag_send.at[h, s],
                 recv_sem=ag_recv.at[h, s],
                 device_id=target,
@@ -338,114 +370,26 @@
             copy.wait()
         bases, length = nexts, 2 * length
 
-
-def front(factor_obs, factor_ctrl, diffusivity, input_map, output_map, ident):
-    nslab, nsub = lax.axis_size("slab"), lax.axis_size("sub")
-    planes, lines, points, wide = factor_ctrl.shape
-    cells = planes * lines * points
-    step = lines * points // (2 if lines % 2 == 0 else 1)
-    rows = wide * (wide // LANES)
-    nfar, turns = far_count(nslab), len(sub_bits(nsub)) + 1
-    half = rows // 2
-    maps = input_map.shape[0] + output_map.shape[0]
-    vmem, anywhere = pl.BlockSpec(memory_space=pltpu.VMEM), pl.BlockSpec(memory_space=pl.ANY)
-    near, far = pltpu.SemaphoreType.DMA((2, turns)), pltpu.SemaphoreType.DMA((2, nfar))
-    f32, bf16 = jnp.float32, jnp.bfloat16
-    return pl.pallas_call(
-        functools.partial(front_kernel, nslab, nsub, points),
-        out_shape=[
-            jax.ShapeDtypeStruct((rows, LANES), f32),
-            jax.ShapeDtypeStruct((wide, wide), f32),
-            jax.ShapeDtypeStruct((maps, wide), f32),
-        ],
-        in_specs=[anywhere, anywhere, vmem, vmem, vmem],
-        out_specs=[vmem, vmem, vmem],
-        scratch_shapes=[
-            pltpu.VMEM((cells, wide), f32),
-            pltpu.VMEM((cells, wide), f32),
-            pltpu.VMEM((cells, LANES), f32),
-            pltpu.VMEM((step, wide), bf16),
-            pltpu.VMEM((step, wide), bf16),
-            pltpu.VMEM((wide, wide), f32),
-            pltpu.VMEM((rows, LANES), f32),
-            pltpu.VMEM((2, half, LANES), f32),
-            pltpu.VMEM((2, nfar, half // 2**turns // nfar, LANES), f32),
-            pltpu.SemaphoreType.DMA((2, cells // step)),
-            near, near, far, far, far, far, near, near,
-        ],
-        compiler_params=pltpu.CompilerParams(
-            collective_id=ident, has_side_effects=True, vmem_limit_bytes=VMEM_BYTES
-        ),
-    )(
-        factor_obs.reshape(cells, wide),
-        factor_ctrl.reshape(cells, wide),
-        diffusivity,
-        input_map,
-        output_map,
-    )
-
-
-def face_chunks(cells):
-    return 2 if cells % 16 == 0 else 1
-
-
-def back_kernel(nslab, nsub, points, sweeps, *refs):
-    order_ref, gram_ref, start_ref, inner_ref, maps_ref, conduct_ref, obs_hbm, ctrl_hbm = refs[:8]
-    mass_ref, state_ref, in_ref, out_ref = refs[8:12]
-    both_high, both_low, block, left_ref, right_ref, work, turned, face = refs[12:20]
-    obs_z, obs_y, ctrl_z, ctrl_y, send_z, send_y, got_z, got_y = refs[20:28]
-    flat, pack, slots, result = refs[28:32]
-    load, z_send, z_recv, y_send, y_recv, rs_send, rs_recv, ag_send, ag_recv = refs[32:]
-    slab, sub = lax.axis_index("slab"), lax.axis_index("sub")
-    rank, size = start_ref.shape
-    planes, plane_cells = conduct_ref.shape
-    total, me = nslab * nsub, slab * nsub + sub
+    rank, size = start.shape
     chunks = face_chunks(plane_cells)
     chunk = plane_cells // chunks
 
-    def peer(off):
-        other = lax.rem(me + off, total)
-        return other, {"slab": other // nsub, "sub": lax.rem(other, nsub)}
-
-    barrier = pltpu.get_barrier_semaphore()
-
-    def greet(off, carry):
-        pl.semaphore_signal(barrier, inc=1, device_id=peer(off)[1])
-        return carry
-
-    lax.fori_loop(1, total, greet, 0)
-
-    loads = []
-    for which, (source, z_face, y_face) in enumerate(
-        ((ctrl_hbm, ctrl_z, ctrl_y), (obs_hbm, obs_z, obs_y))
-    ):
-        for side in range(2):
-            plane = side * (planes - 1)
-            pairs = [(source.at[pl.ds(plane * plane_cells, plane_cells)], z_face.at[side])]
-            for p in range(planes):
-                first = p * plane_cells + side * (plane_cells - points)
-                pairs.append(
-                    (source.at[pl.ds(first, points)], y_face.at[side, pl.ds(p * points, points)])
-                )
-            for i, (here, there) in enumerate(pairs):
-                loads.append(pltpu.make_async_copy(here, there, load.at[which, side, i]))
-    for copy in loads:
-        copy.start()
+    def edge_lines(ref, side):
+        firsts = [p * plane_cells + side * (plane_cells - points) for p in range(planes)]
+        return jnp.concatenate([ref[first : first + points, :] for first in firsts], axis=0)
 
     for c in range(rank // LANES):
         cols = slice(c * LANES, (c + 1) * LANES)
-        tile = gram_ref[c * rank : (c + 1) * rank, :]
+        tile = whole[c * rank : (c + 1) * rank, :]
         high, low = two_parts(tile)
         both_high[1, :, cols] = high
         both_low[1, :, cols] = low
         high, low = two_parts(tile.T)
         both_high[0, cols, :] = high
         both_low[0, cols, :] = low
-    block[...] = start_ref[...]
     row = lax.broadcasted_iota(jnp.int32, (size, size), 0)
     col = lax.broadcasted_iota(jnp.int32, (size, size), 1)
     eye = (row == col).astype(jnp.float32)
-    pl.semaphore_wait(barrier, total - 1)
 
     places = (("slab", slab, nslab, 1), ("slab", slab, nslab, -1))
     places = places + (("sub", sub, nsub, 1), ("sub", sub, nsub, -1))
@@ -479,37 +423,34 @@
         return fold(narrow(high, parts) + narrow(low, parts), size)
 
     def send_faces():
-        parts = pair(apply_parts(both_high[1], both_low[1], block[...]))
+        parts = pair(apply_parts(both_high[1], both_low[1], left[...]))
         image = narrow(both_high[0], parts) + narrow(both_low[0], parts)
         parts = pair(fold(image, size))
-        for copy in loads[: len(loads) // 2]:
-            copy.wait()
         for c in range(chunks):
             for m in range(2):
-                rows = slice(c * chunk, (c + 1) * chunk)
-                send_z[m, c] = project(ctrl_z[1 - m, rows, :], parts)
+                first = (1 - m) * (planes - 1) * plane_cells + c * chunk
+                send_z[m, c] = project(ctrl[first : first + chunk, :], parts)
 
                 @pl.when(beside(m, 1))
                 def _():
                     copy_z(m, c).start()
 
         for m in range(2):
-            send_y[m] = project(ctrl_y[1 - m], parts)
+            send_y[m] = project(edge_lines(ctrl, 1 - m), parts)
 
             @pl.when(beside(2 + m, 1))
             def _():
                 copy_y(m).start()
 
-    def step(k, carry):
+    def sweep(k, carry):
         turn = lax.rem(k, 2)
-        parts = pair(apply_parts(both_high[turn], both_low[turn], block[...]))
-        work[:, :size] = gram_parts(parts)
-        work[:, size:] = eye
-        inverse_factor(work, size)
-        right_ref[...] = left_ref[...]
-        basis = right_apply(parts, work[:, size:])
-        block[...] = basis
-        left_ref[...] = basis
+        parts = pair(apply_parts(both_high[turn], both_low[turn], left[...]))
+        square[:, :size] = gram_parts(parts)
+        square[:, size:] = eye
+        inverse_factor(square, size)
+        right[...] = left[...]
+        basis = right_apply(parts, square[:, size:])
+        left[...] = basis
 
         @pl.when(k == 2 * sweeps - 4)
         def _():
@@ -518,40 +459,27 @@
 
         @pl.when(jnp.logical_and(k > 2 * sweeps - 4, k < 2 * sweeps - 1))
         def _():
-            turned[...] = exact(turned[...], work[:, size:], ((1,), (1,)))
+            turned[...] = exact(turned[...], square[:, size:], ((1,), (1,)))
 
         return carry
 
-    left_ref[...] = start_ref[...]
-    lax.fori_loop(0, 2 * sweeps, step, 0)
-
-    left_parts, right_parts = pair(left_ref[...]), pair(right_ref[...])
+    left[...] = start[...]
+    lax.fori_loop(0, 2 * sweeps, sweep, 0)
+
+    left_parts, right_parts = pair(left[...]), pair(right[...])
     image = fold(narrow(both_high[1], right_parts) + narrow(both_low[1], right_parts), size)
-    kept = order_ref[0]
-    square = jnp.where(jnp.logical_and(row < kept, col < kept), 1.0, 0.0)
-    mass_ref[...] = square * exact(left_ref[...], image, ((0,), (0,)))
-    state = exact(left_ref[...], project(inner_ref[...], right_parts), ((0,), (0,)))
-    maps = maps_ref.shape[0]
-    ins = in_ref.shape[1]
-    seen = project(maps_ref[...], left_parts)
-    felt = project(maps_ref[...], right_parts)
+    out_ref[:size, :] = exact(left[...], image, ((0,), (0,)))
+    state = exact(left[...], project(inner[...], right_parts), ((0,), (0,)))
+    ins, both_maps = drive.shape[0], maps.shape[0]
+    seen = project(maps[...], left_parts)
+    felt = project(maps[...], right_parts)
     side = lax.broadcasted_iota(jnp.int32, seen.shape, 0)
-    flat[...] = jnp.zeros_like(flat)
-    flat[size : size + maps, :] = jnp.where(side < ins, seen, felt)
-    for copy in loads[len(loads) // 2 :]:
-        copy.wait()
-
-    def spread(plane, group):
-        lanes = conduct_ref[plane : plane + 1, group * LANES : (group + 1) * LANES] * (1.0 / 6.0)
-        return jnp.broadcast_to(lanes, (LANES, LANES)).T
-
-    groups = plane_cells // LANES
+    out_ref[2 * size :, :] = jnp.zeros((out_ref.shape[0] - 2 * size, size), jnp.float32)
+    out_ref[2 * size : 2 * size + both_maps, :] = jnp.where(side < ins, seen, felt)
+
     face[...] = jnp.zeros_like(face)
     for m in range(2):
-        mine = project(obs_y[m], left_parts)
-        last = [spread(p, m * (groups - 1)) for p in range(planes)]
-        scale = [part[LANES - points :] if m else part[:points] for part in last]
-        mine = mine * jnp.concatenate(scale, axis=0)
+        mine = project(edge_lines(obs, m), left_parts) * edge_lines(spread_k, m)
 
         @pl.when(beside(2 + m, -1))
         def _():
@@ -560,31 +488,29 @@
 
     for c in range(chunks):
         for m in range(2):
-            rows = slice(c * chunk, (c + 1) * chunk)
-            mine = project(obs_z[m, rows, :], left_parts)
-            per = groups // chunks
-            scale = [spread(m * (planes - 1), c * per + g) for g in range(per)]
-            mine = mine * jnp.concatenate(scale, axis=0)
+            first = m * (planes - 1) * plane_cells + c * chunk
+            rows = slice(first, first + chunk)
+            mine = project(obs[rows, :], left_parts) * spread_k[rows, :]
 
             @pl.when(beside(m, -1))
             def _():
                 copy_z(m, c).wait_recv()
                 face[...] += three_dots(mine, got_z[m, c], ((0,), (0,)))
 
-    flat[:size, :] = state + exact(face[...], turned[...])
+    out_ref[size : 2 * size, :] = state + exact(face[...], turned[...])
     part = pack.shape[1]
-    owners = -(-(size + maps) // part)
+    owners = (out_ref.shape[0] - size) // part
     pack[...] = jnp.zeros_like(pack)
     for d in range(owners):
-        pack[d] = flat[d * part : (d + 1) * part, :]
+        pack[d] = out_ref[size + d * part : size + (d + 1) * part, :]
 
     def gather(off):
         other, target = peer(off)
         return pltpu.make_async_remote_copy(
             src_ref=pack.at[other],
             dst_ref=slots.at[off],
-            send_sem=rs_send.at[off],
-            recv_sem=rs_recv.at[off],
+            send_sem=sum_send.at[off],
+            recv_sem=sum_recv.at[off],
             device_id=target,
         )
 
@@ -592,8 +518,8 @@
         return pltpu.make_async_remote_copy(
             src_ref=result.at[me],
             dst_ref=result.at[me],
-            send_sem=ag_send.at[off],
-            recv_sem=ag_recv.at[off],
+            send_sem=give_send.at[off],
+            recv_sem=give_recv.at[off],
             device_id=peer(off)[1],
         )
 
@@ -602,7 +528,7 @@
             act(off)
             return carry
 
-        lax.fori_loop(1, total, body, 0)
+        lax.fori_loop(1, everyone, body, 0)
 
     loop(lambda off: gather(off).start())
     slots[0] = pack[me]
@@ -623,80 +549,105 @@
 
     loop(lambda off: spread_out(off).wait())
     for d in range(owners):
-        flat[d * part : (d + 1) * part, :] = result[d]
-    state_ref[...] = square * flat[:size, :]
-    lanes = jnp.where(col[:maps, :] < kept, 1.0, 0.0) * flat[size : size + maps, :]
+        out_ref[size + d * part : size + (d + 1) * part, :] = result[d]
+
+
+def finish_kernel(order_ref, raw_ref, mass_ref, state_ref, in_ref, out_ref):
+    size, ins = in_ref.shape
+    outs = out_ref.shape[0]
+    kept = order_ref[0]
+    row = lax.broadcasted_iota(jnp.int32, (size, size), 0)
+    col = lax.broadcasted_iota(jnp.int32, (size, size), 1)
+    square = jnp.where(jnp.logical_and(row < kept, col < kept), 1.0, 0.0)
+    mass_ref[...] = square * raw_ref[:size, :]
+    state_ref[...] = square * raw_ref[size : 2 * size, :]
+    lanes = jnp.where(col[: ins + outs, :] < kept, 1.0, 0.0)
+    lanes = lanes * raw_ref[2 * size : 2 * size + ins + outs, :]
     in_ref[...] = lanes.T[:, :ins]
     out_ref[...] = lanes[ins:, :]
 
 
-def back(order, gram, start, inner, maps, diffusivity, factor_obs, factor_ctrl, ins, ident):
+def on_device(factor_obs, factor_ctrl, diffusivity, input_map, output_map, start_block, order):
     nslab, nsub = lax.axis_size("slab"), lax.axis_size("sub")
     planes, lines, points, wide = factor_ctrl.shape
     cells, plane_cells = planes * lines * points, lines * points
-    rank, size = start.shape
-    total = nslab * nsub
-    rows = size + maps.shape[0]
-    part = -(-rows // total)
+    rank, size = start_block.shape
+    ins, outs = input_map.shape[0], output_map.shape[0]
+    everyone = nslab * nsub
+    step = plane_cells // (2 if lines % 2 == 0 else 1)
+    rows = wide * (wide // LANES)
+    half = rows // 2
+    nfar, turns = far_count(nslab), len(sub_bits(nsub)) + 1
+    part = -(-(size + ins + outs) // everyone)
+    owners = -(-(size + ins + outs) // part)
     chunks = face_chunks(plane_cells)
     side = planes * points
     f32, bf16 = jnp.float32, jnp.bfloat16
     vmem, anywhere = pl.BlockSpec(memory_space=pltpu.VMEM), pl.BlockSpec(memory_space=pl.ANY)
-    every = pltpu.SemaphoreType.DMA((total,))
+    near, far = pltpu.SemaphoreType.DMA((2, turns)), pltpu.SemaphoreType.DMA((2, nfar))
+    every = pltpu.SemaphoreType.DMA((everyone,))
     zs, ys = pltpu.SemaphoreType.DMA((2, chunks)), pltpu.SemaphoreType.DMA((2,))
     faces_z = pltpu.VMEM((2, chunks, plane_cells // chunks, size), f32)
     faces_y = pltpu.VMEM((2, side, size), f32)
-    return pl.pallas_call(
-        functools.partial(back_kernel, nslab, nsub, points, 2),
-        out_shape=[
-            jax.ShapeDtypeStruct((size, size), f32),
-            jax.ShapeDtypeStruct((size, size), f32),
-            jax.ShapeDtypeStruct((size, ins), f32),
-            jax.ShapeDtypeStruct((maps.shape[0] - ins, size), f32),
-        ],
-        in_specs=[pl.BlockSpec(memory_space=pltpu.SMEM)] + [vmem] * 5 + [anywhere] * 2,
-        out_specs=[vmem] * 4,
+    pieces = pltpu.VMEM((everyone, part, LANES), f32)
+    raw = pl.pallas_call(
+        functools.partial(whole_kernel, nslab, nsub, points, 2),
+        out_shape=jax.ShapeDtypeStruct((size + owners * part, size), f32),
+        in_specs=[anywhere] * 6,
+        out_specs=vmem,
         scratch_shapes=[
+            pltpu.VMEM((cells, wide), f32),
+            pltpu.VMEM((cells, wide), f32),
+            pltpu.VMEM((planes, plane_cells), f32),
+            pltpu.VMEM(input_map.shape, f32),
+            pltpu.VMEM(output_map.shape, f32),
+            pltpu.VMEM((rank, size), f32),
+            pltpu.VMEM((cells, LANES), f32),
+            pltpu.VMEM((step, wide), bf16),
+            pltpu.VMEM((step, wide), bf16),
+            pltpu.VMEM((wide, wide), f32),
+            pltpu.VMEM((wide, wide), f32),
+            pltpu.VMEM((ins + outs, wide), f32),
+            pltpu.VMEM((rows, LANES), f32),
+            pltpu.VMEM((2, half, LANES), f32),
+            pltpu.VMEM((2, nfar, half // 2**turns // nfar, LANES), f32),
+            pltpu.VMEM((rows, LANES), f32),
             pltpu.VMEM((2, rank, rank), bf16),
             pltpu.VMEM((2, rank, rank), bf16),
-            pltpu.VMEM((rank, size), f32),
             pltpu.VMEM((rank, size), f32),
             pltpu.VMEM((rank, size), f32),
             pltpu.VMEM((size, 2 * size), f32),
             pltpu.VMEM((size, size), f32),
             pltpu.VMEM((size, size), f32),
-            pltpu.VMEM((2, plane_cells, wide), f32),
-            pltpu.VMEM((2, side, wide), f32),
-            pltpu.VMEM((2, plane_cells, wide), f32),
-            pltpu.VMEM((2, side, wide), f32),
-            faces_z, faces_y, faces_z, faces_y,
-            pltpu.VMEM((part * -(-rows // part), LANES), f32),
-            pltpu.VMEM((total, part, LANES), f32),
-            pltpu.VMEM((total, part, LANES), f32),
-            pltpu.VMEM((total, part, LANES), f32),
-            pltpu.SemaphoreType.DMA((2, 2, planes + 1)),
+            faces_z, faces_y, faces_z, faces_y, pieces, pieces, pieces,
+            pltpu.SemaphoreType.DMA((2, cells // step)),
+            pltpu.SemaphoreType.DMA((4,)),
+            near, near, far, far, far, far, near, near,
             zs, zs, ys, ys, every, every, every, every,
         ],
         compiler_params=pltpu.CompilerParams(
-            collective_id=ident, has_side_effects=True, vmem_limit_bytes=VMEM_BYTES
+            collective_id=0, has_side_effects=True, vmem_limit_bytes=VMEM_BYTES
         ),
     )(
-        order,
-        gram,
-        start,
-        inner,
-        maps,
-        diffusivity,
         factor_obs.reshape(cells, wide),
         factor_ctrl.reshape(cells, wide),
+        diffusivity,
+        input_map,
+        output_map,
+        start_block,
     )
-
-
-def on_device(factor_obs, factor_ctrl, diffusivity, input_map, output_map, start_block, order):
-    gram, inner, maps = front(factor_obs, factor_ctrl, diffusivity, input_map, output_map, 0)
-    ins = input_map.shape[0]
     return tuple(
-        back(order, gram, start_block, inner, maps, diffusivity, factor_obs, factor_ctrl, ins, 1)
+        pl.pallas_call(
+            finish_kernel,
+            out_shape=[
+                jax.ShapeDtypeStruct((size, size), f32),
+                jax.ShapeDtypeStruct((size, size), f32),
+                jax.ShapeDtypeStruct((size, ins), f32),
+                jax.ShapeDtypeStruct((outs, size), f32),
+            ],
+            in_specs=[pl.BlockSpec(memory_space=pltpu.SMEM), vmem],
+            out_specs=[vmem] * 4,
+        )(order, raw)
     )
 
 

time: 101 us -> 93.8 us (0.929)
  local copies, waits for them, and re-layouts: 5.68 us -> 1.49 us
  Pallas kernels: 93.7 us -> 90.8 us
    unnamed x3 -> x0, local copies, waits for them, and re-layouts: 4.19 us -> none
    pallas_call x2, Pallas kernels: 93.7 us -> 90.8 us  [the longest x1 89.1 us: on_device(): pl.pallas_call(functools.partial(whole_kernel, nslab, nsub, points, 2), o...]
where the time goes in v3:
time: 93.8 us; the launch traced here: 93.6 us
  Pallas kernels  90.8 us (97%)
  local copies, waits for them, and re-layouts  1.49 us (2%)
  between operations  1.29 us (1%)
    pallas_call x1, Pallas kernels, on_device(): pl.pallas_call(functools.partial(whole_kernel, nslab, nsub, points, 2), o...  89.1 us

profile of v3, /device:TPU:0, one launch (start us, length us, event | category | flops | bytes accessed | tf_op | source)
XLA Modules:
  0.0 93.6 jit_solution(14408336085952989371)
XLA Ops:
  1.3 89.1 %shard_map.102.raw_ref = f32[268,128]{1,0:T(8,128)} custom-call(f32[4096,512]{1,0:T(8,128)} %bitcast.2, f32[4096,512]{1,0:T(8,128)} %bitcast.3, f32[4,1024]{1,0:T(4,128)} %refs_2_.1, f32[4,4,1024]{2,1,0:T(4,128)} %refs_3_.1, f32[4,4,1024]{2,1,0:T(4,128)} %refs_4_.1, f32[512,128]{1,0:T(8,128)} %refs_5_.1), custom_call_target="tpu_custom_call" | custom-call | tf_op jit(solution)/shard_map/pallas_call | solution.py:593
  90.4 1.6 %shard_map.103 = (f32[128,128]{1,0:T(8,128)}, f32[128,128]{1,0:T(8,128)}, f32[128,4]{1,0:T(8,128)}, f32[4,128]{1,0:T(4,128)}) custom-call(s32[1]{0:T(128)S(6)} %copy.12.order_ref, f32[268,128]{1,0:T(8,128)} %shard_map.102.raw_ref), custom_call_target="tpu_custom_call" | custom-call | tf_op jit(solution)/shard_map/pallas_call | solution.py:640
  92.1 1.5 %copy.11 = f32[128,4]{0,1:T(4,128)} copy(f32[128,4]{1,0:T(8,128)} %get-tuple-element.6) | data formatting | bytes 4096 | tf_op jit(solution)/shard_map/pallas_call | solution.py:640

commit v4 on v3

--- a/solution.py
+++ b/solution.py
@@ -10,6 +10,7 @@
 SUBS = 8
 PANEL = 16
 VMEM_BYTES = 60 * 1024 * 1024
+EARLY_LINES = 2
 HIGHEST = lax.Precision.HIGHEST
 
 
@@ -155,12 +156,19 @@
 def whole_kernel(nslab, nsub, points, sweeps, *refs):
     obs_hbm, ctrl_hbm, conduct_hbm, drive_hbm, sense_hbm, start_hbm, out_ref = refs[:7]
     obs, ctrl, conduct, drive, sense, start, spread_k, applied_high, applied_low = refs[7:16]
-    acc, inner, maps, work, got, got_far, whole = refs[16:23]
-    both_high, both_low, left, right, square, turned, face = refs[23:30]
-    send_z, send_y, got_z, got_y, pack, slots, result = refs[30:37]
-    load, load_small = refs[37:39]
-    rs_send, rs_recv, far_send, far_recv, back_send, back_recv, ag_send, ag_recv = refs[39:47]
-    z_send, z_recv, y_send, y_recv, sum_send, sum_recv, give_send, give_recv = refs[47:]
+    turns = [("sub", bit) for bit in sub_bits(nsub)] + [("slab", 1)]
+    refs = list(refs[16:])
+
+    def take(count):
+        return [refs.pop(0) for _ in range(count)]
+
+    acc, inner, maps, work, whole, got_far = take(6)
+    got = take(len(turns))
+    both_high, both_low, left, right, square, turned, face = take(7)
+    send_z, send_y, got_z, got_y, pack, slots, result = take(7)
+    raw_z, load, load_small, raw_send, raw_recv = take(5)
+    rs_send, rs_recv, far_send, far_recv, back_send, back_recv, ag_send, ag_recv = take(8)
+    z_send, z_recv, y_send, y_recv, sum_send, sum_recv, give_send, give_recv = take(8)
     slab, sub = lax.axis_index("slab"), lax.axis_index("sub")
     everyone, me, peer = peers(slab, sub, nslab, nsub)
     cells, wide = ctrl.shape
@@ -168,14 +176,30 @@
     step = applied_high.shape[0]
     count = cells // step
     nfar = far_count(nslab)
-    turns = [("sub", bit) for bit in sub_bits(nsub)] + [("slab", 1)]
-    orders = (turns, turns[:1] + turns[1:][::-1])
 
     def fetch(which, k):
         rows = pl.ds(k * step, step)
         source, target = ((obs_hbm, obs), (ctrl_hbm, ctrl))[which]
         return pltpu.make_async_copy(source.at[rows], target.at[rows], load.at[which, k])
 
+    places = (("slab", slab, nslab, 1), ("slab", slab, nslab, -1))
+    places = places + (("sub", sub, nsub, 1), ("sub", sub, nsub, -1))
+
+    def beside(m, way):
+        _, index, count, step = places[m]
+        return index < count - 1 if step * way > 0 else index > 0
+
+    def copy_raw(m):
+        axis, index, _, way = places[m]
+        first = (1 - m) * (planes - 1) * plane_cells
+        return pltpu.make_async_remote_copy(
+            src_ref=ctrl_hbm.at[pl.ds(first, raw_z.shape[1])],
+            dst_ref=raw_z.at[m],
+            send_sem=raw_send.at[m],
+            recv_sem=raw_recv.at[m],
+            device_id={axis: index + way},
+        )
+
     small = [
         pltpu.make_async_copy(here, there, load_small.at[i])
         for i, (here, there) in enumerate(
@@ -183,7 +207,8 @@
         )
     ]
     small[0].start()
-    for k in range(count):
+    ahead = min(2, count)
+    for k in range(ahead):
         fetch(0, k).start()
         fetch(1, k).start()
     for copy in small[1:]:
@@ -216,17 +241,34 @@
     def add_block(k, carry):
         fetch(0, k).wait()
         fetch(1, k).wait()
+
+        @pl.when(k + ahead < count)
+        def _():
+            fetch(0, k + ahead).start()
+            fetch(1, k + ahead).start()
+
         rows = pl.ds(pl.multiple_of(k * step, step), step)
-        acc[...] += three_dots(obs[rows, :], ctrl[rows, :], ((0,), (0,)))
+        acc[...] += three_dots(ctrl[rows, :], obs[rows, :], ((0,), (0,)))
         return carry
 
-    lax.fori_loop(0, count, add_block, 0)
-    tall_rows = acc.shape[0]
+    lax.fori_loop(0, 1, add_block, 0)
+    pl.semaphore_wait(barrier, everyone - 1)
+    for m in range(2):
+
+        @pl.when(beside(m, 1))
+        def _():
+            copy_raw(m).start()
+
+        @pl.when(jnp.logical_not(beside(m, -1)))
+        def _():
+            raw_z[m] = jnp.zeros(raw_z.shape[1:], jnp.float32)
+
+    lax.fori_loop(1, count, add_block, 0)
+    blocked = work.shape[1:]
     for c in range(acc.shape[1] // LANES):
-        work[c * tall_rows : (c + 1) * tall_rows, :] = acc[:, c * LANES : (c + 1) * LANES]
+        work[c] = acc[:, c * LANES : (c + 1) * LANES].reshape(blocked)
     for copy in small[1:]:
         copy.wait()
-    pl.semaphore_wait(barrier, everyone - 1)
 
     place = lax.broadcasted_iota(jnp.int32, (points, wide), 0)
 
@@ -234,7 +276,15 @@
         first = k * step
         plane = first // plane_cells
 
-        def line(i, carry):
+        ends = ((0, 0), (1, planes - 1))
+        sides = [m for m, at in ends if at == plane and first % plane_cells == 0]
+        for m in sides:
+
+            @pl.when(beside(m, -1))
+            def _():
+                copy_raw(m).wait_recv()
+
+        def line(i, carry, sides=()):
             row = pl.multiple_of(first + i * points, points)
             within = lax.rem(row, plane_cells)
             here = ctrl[pl.ds(row, points), :]
@@ -249,13 +299,18 @@
                 total = total + ctrl[pl.ds(row - plane_cells, points), :]
             if plane < planes - 1:
                 total = total + ctrl[pl.ds(row + plane_cells, points), :]
+            for m in sides:
+                total = total + raw_z[m, pl.ds(pl.multiple_of(i * points, points), points), :]
             scale = jnp.concatenate([spread_k[pl.ds(row, points), :]] * (wide // LANES), axis=1)
             high, low = two_parts(scale * (total - 6.0 * here))
             applied_high[pl.ds(pl.multiple_of(i * points, points), points), :] = high
             applied_low[pl.ds(pl.multiple_of(i * points, points), points), :] = low
             return carry
 
-        lax.fori_loop(0, step // points, line, 0)
+        extra = raw_z.shape[1] // points if sides else 0
+        if sides:
+            lax.fori_loop(0, extra, functools.partial(line, sides=sides), 0)
+        lax.fori_loop(extra, step // points, line, 0)
         rows = slice(first, first + step)
         high, low = two_parts(obs[rows, :])
         dims = ((0,), (0,))
@@ -266,14 +321,17 @@
         seen = three_dots(drive[:, plane, lanes], obs[rows, :])
         felt = three_dots(sense[:, plane, lanes], ctrl[rows, :])
         both = jnp.concatenate([seen, felt], axis=0)
-        if k == 0:
+        if k == sequence[0]:
             inner[...] = value
             maps[...] = both
         else:
             inner[...] += value
             maps[...] += both
 
-    blocks = iter(range(count))
+    per_plane = plane_cells // step
+    late = [0, (planes - 1) * per_plane]
+    sequence = [k for k in range(count) if k not in late] + late
+    blocks = iter(sequence)
 
     def work_meanwhile(amount):
         for _ in range(amount):
@@ -281,122 +339,117 @@
             if k is not None:
                 inner_block(k)
 
-    gaps = 2 * len(turns) + 2
-    share = -(-count // gaps)
-    rows = work.shape[0]
-    length = rows // 2
-    bases, taken = [0, length], 0
+    share = -(-count // (2 * len(turns) + 2))
+    tiles = work.shape[0]
+    here = [partner(axis, bit)[0] for axis, bit in turns]
+    orders = [list(range(len(turns))) for _ in range(tiles)]
+    for c in range(1, tiles, 2):
+        orders[c] = orders[c][:1] + orders[c][1:][::-1]
+
+    def region(c, done, flip=None):
+        index = [slice(None)] * len(turns)
+        for t in done:
+            index[t] = here[t]
+        if flip is not None:
+            index[flip] = 1 - here[flip]
+        return (c, *index)
+
+    def halve(c, s):
+        t = orders[c][s]
+        return pltpu.make_async_remote_copy(
+            src_ref=work.at[region(c, orders[c][:s], t)],
+            dst_ref=got[s].at[c],
+            send_sem=rs_send.at[c, s],
+            recv_sem=rs_recv.at[c, s],
+            device_id=partner(*turns[t])[1],
+        )
+
+    def scatter(c, off):
+        other, target = far(off)
+        return pltpu.make_async_remote_copy(
+            src_ref=work.at[(c, *here, other)],
+            dst_ref=got_far.at[c, off],
+            send_sem=far_send.at[c, off],
+            recv_sem=far_recv.at[c, off],
+            device_id=target,
+        )
+
+    def gather_far(c, off):
+        return pltpu.make_async_remote_copy(
+            src_ref=whole.at[(c, *here, slab // 2)],
+            dst_ref=whole.at[(c, *here, slab // 2)],
+            send_sem=back_send.at[c, off],
+            recv_sem=back_recv.at[c, off],
+            device_id=far(off)[1],
+        )
+
+    def double(c, s):
+        mine = region(c, orders[c][: s + 1])
+        return pltpu.make_async_remote_copy(
+            src_ref=whole.at[mine],
+            dst_ref=whole.at[mine],
+            send_sem=ag_send.at[c, s],
+            recv_sem=ag_recv.at[c, s],
+            device_id=partner(*turns[orders[c][s]])[1],
+        )
+
+    last = len(turns) - 1
     for s in range(len(turns)):
-        length = length // 2
-        copies, keeps = [], []
-        for h in range(2):
-            axis, bit = orders[h][s]
-            has, target = partner(axis, bit)
-            keeps.append(pl.multiple_of(bases[h] + has * length, 8))
-            give = pl.multiple_of(bases[h] + (1 - has) * length, 8)
-            copies.append(
-                pltpu.make_async_remote_copy(
-                    src_ref=work.at[pl.ds(give, length)],
-                    dst_ref=got.at[h, pl.ds(taken, length)],
-                    send_sem=rs_send.at[h, s],
-                    recv_sem=rs_recv.at[h, s],
-                    device_id=target,
-                )
-            )
-            copies[h].start()
+        for c in range(tiles):
+            if s:
+                halve(c, s - 1).wait()
+                work[region(c, orders[c][:s])] += got[s - 1][c]
+            halve(c, s).start()
         work_meanwhile(share)
-        for h in range(2):
-            copies[h].wait()
-            work[pl.ds(keeps[h], length), :] += got[h, taken : taken + length, :]
-        bases, taken = keeps, taken + length
-
-    piece = length // nfar
-    mines = [pl.multiple_of(bases[h] + (slab // 2) * piece, 8) for h in range(2)]
-    copies = []
-    for h in range(2):
+    for c in range(tiles):
+        halve(c, last).wait()
+        work[(c, *here)] += got[last][c]
         for off in range(1, nfar):
-            other, target = far(off)
-            copy = pltpu.make_async_remote_copy(
-                src_ref=work.at[pl.ds(pl.multiple_of(bases[h] + other * piece, 8), piece)],
-                dst_ref=got_far.at[h, off],
-                send_sem=far_send.at[h, off],
-                recv_sem=far_recv.at[h, off],
-                device_id=target,
-            )
-            copy.start()
-            copies.append(copy)
+            scatter(c, off).start()
     work_meanwhile(share)
-    for copy in copies:
-        copy.wait()
-    for h in range(2):
-        total = work[pl.ds(mines[h], piece), :]
+    for c in range(tiles):
+        total = work[(c, *here, slab // 2)]
         for off in range(1, nfar):
-            total = total + got_far[h, off]
-        whole[pl.ds(mines[h], piece), :] = total
-
-    copies = []
-    for h in range(2):
+            scatter(c, off).wait()
+            total = total + got_far[c, off]
+        whole[(c, *here, slab // 2)] = total
         for off in range(1, nfar):
-            copy = pltpu.make_async_remote_copy(
-                src_ref=whole.at[pl.ds(mines[h], piece)],
-                dst_ref=whole.at[pl.ds(mines[h], piece)],
-                send_sem=back_send.at[h, off],
-                recv_sem=back_recv.at[h, off],
-                device_id=far(off)[1],
-            )
-            copy.start()
-            copies.append(copy)
+            gather_far(c, off).start()
     work_meanwhile(share)
-    for copy in copies:
-        copy.wait()
-
     for s in reversed(range(len(turns))):
-        copies, nexts = [], []
-        for h in range(2):
-            axis, bit = orders[h][s]
-            has, target = partner(axis, bit)
-            copy = pltpu.make_async_remote_copy(
-                src_ref=whole.at[pl.ds(bases[h], length)],
-                dst_ref=whole.at[pl.ds(bases[h], length)],
-                send_sem=ag_send.at[h, s],
-                recv_sem=ag_recv.at[h, s],
-                device_id=target,
-            )
-            copy.start()
-            copies.append(copy)
-            nexts.append(pl.multiple_of(bases[h] - has * length, 8))
+        for c in range(tiles):
+            if s == last:
+                for off in range(1, nfar):
+                    gather_far(c, off).wait()
+            else:
+                double(c, s + 1).wait()
+            double(c, s).start()
         work_meanwhile(share if s else count)
-        for copy in copies:
-            copy.wait()
-        bases, length = nexts, 2 * length
+    for c in range(tiles):
+        double(c, 0).wait()
 
     rank, size = start.shape
     chunks = face_chunks(plane_cells)
-    chunk = plane_cells // chunks
+    early = raw_z.shape[1]
+    chunk = (plane_cells - early) // chunks
 
     def edge_lines(ref, side):
         firsts = [p * plane_cells + side * (plane_cells - points) for p in range(planes)]
         return jnp.concatenate([ref[first : first + points, :] for first in firsts], axis=0)
 
-    for c in range(rank // LANES):
+    for c in range(tiles):
         cols = slice(c * LANES, (c + 1) * LANES)
-        tile = whole[c * rank : (c + 1) * rank, :]
+        tile = whole[c].reshape(rank, LANES)
         high, low = two_parts(tile)
-        both_high[1, :, cols] = high
-        both_low[1, :, cols] = low
+        both_high[0, :, cols] = high
+        both_low[0, :, cols] = low
         high, low = two_parts(tile.T)
-        both_high[0, cols, :] = high
-        both_low[0, cols, :] = low
+        both_high[1, cols, :] = high
+        both_low[1, cols, :] = low
+    left[...] = start[...]
     row = lax.broadcasted_iota(jnp.int32, (size, size), 0)
     col = lax.broadcasted_iota(jnp.int32, (size, size), 1)
     eye = (row == col).astype(jnp.float32)
-
-    places = (("slab", slab, nslab, 1), ("slab", slab, nslab, -1))
-    places = places + (("sub", sub, nsub, 1), ("sub", sub, nsub, -1))
-
-    def beside(m, way):
-        _, index, count, step = places[m]
-        return index < count - 1 if step * way > 0 else index > 0
 
     def copy_z(m, c):
         axis, index, _, step = places[m]
@@ -428,7 +481,7 @@
         parts = pair(fold(image, size))
         for c in range(chunks):
             for m in range(2):
-                first = (1 - m) * (planes - 1) * plane_cells + c * chunk
+                first = (1 - m) * (planes - 1) * plane_cells + early + c * chunk
                 send_z[m, c] = project(ctrl[first : first + chunk, :], parts)
 
                 @pl.when(beside(m, 1))
@@ -463,7 +516,6 @@
 
         return carry
 
-    left[...] = start[...]
     lax.fori_loop(0, 2 * sweeps, sweep, 0)
 
     left_parts, right_parts = pair(left[...]), pair(right[...])
@@ -488,7 +540,7 @@
 
     for c in range(chunks):
         for m in range(2):
-            first = m * (planes - 1) * plane_cells + c * chunk
+            first = m * (planes - 1) * plane_cells + early + c * chunk
             rows = slice(first, first + chunk)
             mine = project(obs[rows, :], left_parts) * spread_k[rows, :]
 
@@ -498,44 +550,60 @@
                 face[...] += three_dots(mine, got_z[m, c], ((0,), (0,)))
 
     out_ref[size : 2 * size, :] = state + exact(face[...], turned[...])
-    part = pack.shape[1]
-    owners = (out_ref.shape[0] - size) // part
-    pack[...] = jnp.zeros_like(pack)
+    owners, part = pack.shape[:2]
+    lead = (nslab // 4) * nsub
+    rank_of = me - lead
+    owning = jnp.logical_and(rank_of >= 0, rank_of < owners)
     for d in range(owners):
         pack[d] = out_ref[size + d * part : size + (d + 1) * part, :]
 
-    def gather(off):
-        other, target = peer(off)
-        return pltpu.make_async_remote_copy(
-            src_ref=pack.at[other],
-            dst_ref=slots.at[off],
-            send_sem=sum_send.at[off],
-            recv_sem=sum_recv.at[off],
-            device_id=target,
-        )
-
-    def spread_out(off):
-        return pltpu.make_async_remote_copy(
-            src_ref=result.at[me],
-            dst_ref=result.at[me],
+    def device(linear):
+        return {"slab": linear // nsub, "sub": lax.rem(linear, nsub)}
+
+    def collect(owner, source):
+        return pltpu.make_async_remote_copy(
+            src_ref=pack.at[owner],
+            dst_ref=slots.at[source],
+            send_sem=sum_send.at[owner],
+            recv_sem=sum_recv.at[source],
+            device_id=device(lead + owner),
+        )
+
+    def hand_out(owner, off):
+        return pltpu.make_async_remote_copy(
+            src_ref=result.at[owner],
+            dst_ref=result.at[owner],
             send_sem=give_send.at[off],
-            recv_sem=give_recv.at[off],
+            recv_sem=give_recv.at[owner],
             device_id=peer(off)[1],
         )
 
-    def loop(act):
-        def body(off, carry):
-            act(off)
+    def loop(start, stop, act):
+        def body(i, carry):
+            act(i)
             return carry
 
-        lax.fori_loop(1, everyone, body, 0)
-
-    loop(lambda off: gather(off).start())
-    slots[0] = pack[me]
-    loop(lambda off: gather(off).wait())
-    result[me] = jnp.sum(slots[...], axis=0)
-    loop(lambda off: spread_out(off).start())
+        lax.fori_loop(start, stop, body, 0)
+
+    def unless_me(linear, act):
+        @pl.when(linear != me)
+        def _():
+            act()
+
+    loop(0, owners, lambda d: unless_me(lead + d, lambda: collect(d, me).start()))
+
+    @pl.when(owning)
+    def _():
+        slots[me] = pack[rank_of]
+        loop(0, everyone, lambda i: unless_me(i, lambda: collect(0, i).wait_recv()))
+        result[rank_of] = jnp.sum(slots[...], axis=0)
+        loop(1, everyone, lambda off: hand_out(rank_of, off).start())
+
     for m in range(2):
+
+        @pl.when(beside(m, 1))
+        def _():
+            copy_raw(m).wait_send()
 
         @pl.when(beside(2 + m, 1))
         def _():
@@ -547,13 +615,19 @@
             def _():
                 copy_z(m, c).wait_send()
 
-    loop(lambda off: spread_out(off).wait())
+    loop(0, owners, lambda d: unless_me(lead + d, lambda: collect(d, me).wait_send()))
+    loop(0, owners, lambda d: unless_me(lead + d, lambda: hand_out(d, 1).wait_recv()))
+
+    @pl.when(owning)
+    def _():
+        loop(1, everyone, lambda off: hand_out(rank_of, off).wait_send())
+
     for d in range(owners):
         out_ref[size + d * part : size + (d + 1) * part, :] = result[d]
 
 
 def finish_kernel(order_ref, raw_ref, mass_ref, state_ref, in_ref, out_ref):
-    size, ins = in_ref.shape
+    ins, size = in_ref.shape
     outs = out_ref.shape[0]
     kept = order_ref[0]
     row = lax.broadcasted_iota(jnp.int32, (size, size), 0)
@@ -563,7 +637,7 @@
     state_ref[...] = square * raw_ref[size : 2 * size, :]
     lanes = jnp.where(col[: ins + outs, :] < kept, 1.0, 0.0)
     lanes = lanes * raw_ref[2 * size : 2 * size + ins + outs, :]
-    in_ref[...] = lanes.T[:, :ins]
+    in_ref[...] = lanes[:ins, :]
     out_ref[...] = lanes[ins:, :]
 
 
@@ -575,21 +649,23 @@
     ins, outs = input_map.shape[0], output_map.shape[0]
     everyone = nslab * nsub
     step = plane_cells // (2 if lines % 2 == 0 else 1)
-    rows = wide * (wide // LANES)
-    half = rows // 2
     nfar, turns = far_count(nslab), len(sub_bits(nsub)) + 1
-    part = -(-(size + ins + outs) // everyone)
+    tiles, piece = wide // LANES, wide // 2**turns // nfar
+    blocked = pltpu.VMEM((tiles, *(2,) * turns, nfar, piece, LANES), jnp.float32)
+    part = -(-(size + ins + outs) // max(everyone // 2, 1))
     owners = -(-(size + ins + outs) // part)
     chunks = face_chunks(plane_cells)
     side = planes * points
     f32, bf16 = jnp.float32, jnp.bfloat16
     vmem, anywhere = pl.BlockSpec(memory_space=pltpu.VMEM), pl.BlockSpec(memory_space=pl.ANY)
-    near, far = pltpu.SemaphoreType.DMA((2, turns)), pltpu.SemaphoreType.DMA((2, nfar))
+    near, far = pltpu.SemaphoreType.DMA((tiles, turns)), pltpu.SemaphoreType.DMA((tiles, nfar))
     every = pltpu.SemaphoreType.DMA((everyone,))
     zs, ys = pltpu.SemaphoreType.DMA((2, chunks)), pltpu.SemaphoreType.DMA((2,))
-    faces_z = pltpu.VMEM((2, chunks, plane_cells // chunks, size), f32)
+    early = EARLY_LINES * points
+    faces_z = pltpu.VMEM((2, chunks, (plane_cells - early) // chunks, size), f32)
     faces_y = pltpu.VMEM((2, side, size), f32)
     pieces = pltpu.VMEM((everyone, part, LANES), f32)
+    owned = pltpu.VMEM((owners, part, LANES), f32)
     raw = pl.pallas_call(
         functools.partial(whole_kernel, nslab, nsub, points, 2),
         out_shape=jax.ShapeDtypeStruct((size + owners * part, size), f32),
@@ -608,10 +684,14 @@
             pltpu.VMEM((wide, wide), f32),
             pltpu.VMEM((wide, wide), f32),
             pltpu.VMEM((ins + outs, wide), f32),
-            pltpu.VMEM((rows, LANES), f32),
-            pltpu.VMEM((2, half, LANES), f32),
-            pltpu.VMEM((2, nfar, half // 2**turns // nfar, LANES), f32),
-            pltpu.VMEM((rows, LANES), f32),
+            blocked, blocked,
+            pltpu.VMEM((tiles, nfar, piece, LANES), f32),
+        ]
+        + [
+            pltpu.VMEM((tiles, *(2,) * (turns - 1 - s), nfar, piece, LANES), f32)
+            for s in range(turns)
+        ]
+        + [
             pltpu.VMEM((2, rank, rank), bf16),
             pltpu.VMEM((2, rank, rank), bf16),
             pltpu.VMEM((rank, size), f32),
@@ -619,9 +699,11 @@
             pltpu.VMEM((size, 2 * size), f32),
             pltpu.VMEM((size, size), f32),
             pltpu.VMEM((size, size), f32),
-            faces_z, faces_y, faces_z, faces_y, pieces, pieces, pieces,
+            faces_z, faces_y, faces_z, faces_y, owned, pieces, owned,
+            pltpu.VMEM((2, early, wide), f32),
             pltpu.SemaphoreType.DMA((2, cells // step)),
             pltpu.SemaphoreType.DMA((4,)),
+            ys, ys,
             near, near, far, far, far, far, near, near,
             zs, zs, ys, ys, every, every, every, every,
         ],
@@ -636,19 +718,18 @@
         output_map,
         start_block,
     )
-    return tuple(
-        pl.pallas_call(
-            finish_kernel,
-            out_shape=[
-                jax.ShapeDtypeStruct((size, size), f32),
-                jax.ShapeDtypeStruct((size, size), f32),
-                jax.ShapeDtypeStruct((size, ins), f32),
-                jax.ShapeDtypeStruct((outs, size), f32),
-            ],
-            in_specs=[pl.BlockSpec(memory_space=pltpu.SMEM), vmem],
-            out_specs=[vmem] * 4,
-        )(order, raw)
-    )
+    mass, state, seen, felt = pl.pallas_call(
+        finish_kernel,
+        out_shape=[
+            jax.ShapeDtypeStruct((size, size), f32),
+            jax.ShapeDtypeStruct((size, size), f32),
+            jax.ShapeDtypeStruct((ins, size), f32),
+            jax.ShapeDtypeStruct((outs, size), f32),
+        ],
+        in_specs=[pl.BlockSpec(memory_space=pltpu.SMEM), vmem],
+        out_specs=[vmem] * 4,
+    )(order, raw)
+    return mass, state, seen.T, felt
 
 
 def solution(mesh):

time: 93.8 us -> 86 us (0.917)
  Pallas kernels: 90.8 us -> 84.5 us
  local copies, waits for them, and re-layouts: 1.49 us -> 0 us
    pallas_call x1, Pallas kernels: 89.1 us -> 82.9 us  [on_device(): pl.pallas_call(functools.partial(whole_kernel, nslab, nsub, points, 2), o...]
    pallas_call x1 -> x0, local copies, waits for them, and re-layouts: 1.49 us -> none  [on_device(): pl.pallas_call(finish_kernel, out_shape=[jax.ShapeDtypeStruct((size, size...]
where the time goes in v4:
time: 86 us; the launch traced here: 85.8 us
  Pallas kernels  84.5 us (98%)
  between operations  1.29 us (2%)
    pallas_call x1, Pallas kernels, on_device(): pl.pallas_call(functools.partial(whole_kernel, nslab, nsub, points, 2), o...  82.9 us

profile of v4, /device:TPU:0, one launch (start us, length us, event | category | flops | bytes accessed | tf_op | source)
XLA Modules:
  0.0 85.8 jit_solution(9573321539224415597)
XLA Ops:
  1.3 82.9 %shard_map.102.raw_ref = f32[272,128]{1,0:T(8,128)} custom-call(f32[4096,512]{1,0:T(8,128)} %bitcast.3, f32[4096,512]{1,0:T(8,128)} %bitcast.4, f32[4,1024]{1,0:T(4,128)} %refs_2_.1, f32[4,4,1024]{2,1,0:T(4,128)} %refs_3_.1, f32[4,4,1024]{2,1,0:T(4,128)} %refs_4_.1, f32[512,128]{1,0:T(8,128)} %refs_5_.1), custom_call_target="tpu_custom_call" | custom-call | tf_op jit(solution)/shard_map/pallas_call | solution.py:669
  84.2 1.6 %shard_map.103 = (f32[128,128]{1,0:T(8,128)}, f32[128,128]{1,0:T(8,128)}, f32[4,128]{1,0:T(4,128)}, f32[4,128]{1,0:T(4,128)}) custom-call(s32[1]{0:T(128)S(6)} %copy.11.order_ref, f32[272,128]{1,0:T(8,128)} %shard_map.102.raw_ref), custom_call_target="tpu_custom_call" | custom-call | tf_op jit(solution)/shard_map/pallas_call | solution.py:721

commit v5 on v4

--- a/solution.py
+++ b/solution.py
@@ -10,7 +10,8 @@
 SUBS = 8
 PANEL = 16
 VMEM_BYTES = 60 * 1024 * 1024
-EARLY_LINES = 2
+EARLY_LINES = 1
+SHARES = (1, 1, 1, 1, 1, 1)
 HIGHEST = lax.Precision.HIGHEST
 
 
@@ -50,6 +51,14 @@
 
 def face_chunks(cells):
     return 2 if cells % 16 == 0 else 1
+
+
+def thin_dot(rows, high, low):
+    above, below = two_parts(rows)
+    stack = jnp.concatenate([above.astype(jnp.float32), below.astype(jnp.float32)], axis=0)
+    both = narrow(stack.astype(jnp.bfloat16), high)
+    count = rows.shape[0]
+    return both[:count] + (both[count:] + narrow(above, low))
 
 
 def across(block, sub):
@@ -164,9 +173,9 @@
 
     acc, inner, maps, work, whole, got_far = take(6)
     got = take(len(turns))
-    both_high, both_low, left, right, square, turned, face = take(7)
+    both_high, both_low, left, right, product, square, turned, face = take(8)
     send_z, send_y, got_z, got_y, pack, slots, result = take(7)
-    raw_z, load, load_small, raw_send, raw_recv = take(5)
+    raw_z, image0, load, load_small, raw_send, raw_recv, image_send, image_recv = take(8)
     rs_send, rs_recv, far_send, far_recv, back_send, back_recv, ag_send, ag_recv = take(8)
     z_send, z_recv, y_send, y_recv, sum_send, sum_recv, give_send, give_recv = take(8)
     slab, sub = lax.axis_index("slab"), lax.axis_index("sub")
@@ -318,8 +327,8 @@
             narrow(high, applied_low[...], dims) + narrow(low, applied_high[...], dims)
         )
         lanes = slice(first % plane_cells, first % plane_cells + step)
-        seen = three_dots(drive[:, plane, lanes], obs[rows, :])
-        felt = three_dots(sense[:, plane, lanes], ctrl[rows, :])
+        seen = thin_dot(drive[:, plane, lanes], high, low)
+        felt = thin_dot(sense[:, plane, lanes], *two_parts(ctrl[rows, :]))
         both = jnp.concatenate([seen, felt], axis=0)
         if k == sequence[0]:
             inner[...] = value
@@ -339,7 +348,6 @@
             if k is not None:
                 inner_block(k)
 
-    share = -(-count // (2 * len(turns) + 2))
     tiles = work.shape[0]
     here = [partner(axis, bit)[0] for axis, bit in turns]
     orders = [list(range(len(turns))) for _ in range(tiles)]
@@ -400,13 +408,13 @@
                 halve(c, s - 1).wait()
                 work[region(c, orders[c][:s])] += got[s - 1][c]
             halve(c, s).start()
-        work_meanwhile(share)
+        work_meanwhile(SHARES[s])
     for c in range(tiles):
         halve(c, last).wait()
         work[(c, *here)] += got[last][c]
         for off in range(1, nfar):
             scatter(c, off).start()
-    work_meanwhile(share)
+    work_meanwhile(SHARES[-3])
     for c in range(tiles):
         total = work[(c, *here, slab // 2)]
         for off in range(1, nfar):
@@ -415,8 +423,28 @@
         whole[(c, *here, slab // 2)] = total
         for off in range(1, nfar):
             gather_far(c, off).start()
-    work_meanwhile(share)
-    for s in reversed(range(len(turns))):
+
+    def broadcast(off):
+        return pltpu.make_async_remote_copy(
+            src_ref=image0.at[(*here, slab // 2)],
+            dst_ref=image0.at[(*here, slab // 2)],
+            send_sem=image_send.at[off],
+            recv_sem=image_recv.at[off],
+            device_id=peer(off)[1],
+        )
+
+    def loop(first, stop, act):
+        def body(i, carry):
+            act(i)
+            return carry
+
+        lax.fori_loop(first, stop, body, 0)
+
+    slices = [whole[(c, *here, slab // 2)] for c in range(tiles)]
+    image0[(*here, slab // 2)] = three_dots(jnp.concatenate(slices, axis=1), start[...])
+    loop(1, everyone // 2, lambda off: broadcast(2 * off).start())
+
+    def advance(s):
         for c in range(tiles):
             if s == last:
                 for off in range(1, nfar):
@@ -424,9 +452,22 @@
             else:
                 double(c, s + 1).wait()
             double(c, s).start()
-        work_meanwhile(share if s else count)
-    for c in range(tiles):
-        double(c, 0).wait()
+
+    work_meanwhile(SHARES[-2])
+    advance(last)
+    work_meanwhile(SHARES[-1])
+    loop(1, everyone // 2, lambda off: broadcast(2 * off).wait())
+    swap = pltpu.make_async_remote_copy(
+        src_ref=image0.at[here[0]],
+        dst_ref=image0.at[here[0]],
+        send_sem=image_send.at[0],
+        recv_sem=image_recv.at[0],
+        device_id=partner(*turns[0])[1],
+    )
+    swap.start()
+    for s in reversed(range(1, last)):
+        advance(s)
+    swap.wait()
 
     rank, size = start.shape
     chunks = face_chunks(plane_cells)
@@ -437,16 +478,6 @@
         firsts = [p * plane_cells + side * (plane_cells - points) for p in range(planes)]
         return jnp.concatenate([ref[first : first + points, :] for first in firsts], axis=0)
 
-    for c in range(tiles):
-        cols = slice(c * LANES, (c + 1) * LANES)
-        tile = whole[c].reshape(rank, LANES)
-        high, low = two_parts(tile)
-        both_high[0, :, cols] = high
-        both_low[0, :, cols] = low
-        high, low = two_parts(tile.T)
-        both_high[1, cols, :] = high
-        both_low[1, cols, :] = low
-    left[...] = start[...]
     row = lax.broadcasted_iota(jnp.int32, (size, size), 0)
     col = lax.broadcasted_iota(jnp.int32, (size, size), 1)
     eye = (row == col).astype(jnp.float32)
@@ -497,27 +528,48 @@
 
     def sweep(k, carry):
         turn = lax.rem(k, 2)
-        parts = pair(apply_parts(both_high[turn], both_low[turn], left[...]))
+
+        @pl.when(k == 0)
+        def _():
+            product[...] = image0[...].reshape(rank, size)
+
+        @pl.when(k > 0)
+        def _():
+            product[...] = apply_parts(both_high[turn], both_low[turn], left[...])
+
+        parts = pair(product[...])
         square[:, :size] = gram_parts(parts)
         square[:, size:] = eye
         inverse_factor(square, size)
         right[...] = left[...]
-        basis = right_apply(parts, square[:, size:])
-        left[...] = basis
-
-        @pl.when(k == 2 * sweeps - 4)
-        def _():
+        left[...] = right_apply(parts, square[:, size:])
+
+        @pl.when(k == 0)
+        def _():
+            advance(0)
+            for c in range(tiles):
+                double(c, 0).wait()
+                cols = slice(c * LANES, (c + 1) * LANES)
+                tile = whole[c].reshape(rank, LANES)
+                high, low = two_parts(tile)
+                both_high[0, :, cols] = high
+                both_low[0, :, cols] = low
+                high, low = two_parts(tile.T)
+                both_high[1, cols, :] = high
+                both_low[1, cols, :] = low
             send_faces()
             turned[...] = eye
 
-        @pl.when(jnp.logical_and(k > 2 * sweeps - 4, k < 2 * sweeps - 1))
+        @pl.when(jnp.logical_and(k > 0, k < 2 * sweeps - 1))
         def _():
             turned[...] = exact(turned[...], square[:, size:], ((1,), (1,)))
 
         return carry
 
+    left[...] = start[...]
     lax.fori_loop(0, 2 * sweeps, sweep, 0)
 
+    work_meanwhile(count)
     left_parts, right_parts = pair(left[...]), pair(right[...])
     image = fold(narrow(both_high[1], right_parts) + narrow(both_low[1], right_parts), size)
     out_ref[:size, :] = exact(left[...], image, ((0,), (0,)))
@@ -577,13 +629,6 @@
             recv_sem=give_recv.at[owner],
             device_id=peer(off)[1],
         )
-
-    def loop(start, stop, act):
-        def body(i, carry):
-            act(i)
-            return carry
-
-        lax.fori_loop(start, stop, body, 0)
 
     def unless_me(linear, act):
         @pl.when(linear != me)
@@ -696,14 +741,16 @@
             pltpu.VMEM((2, rank, rank), bf16),
             pltpu.VMEM((rank, size), f32),
             pltpu.VMEM((rank, size), f32),
+            pltpu.VMEM((rank, size), f32),
             pltpu.VMEM((size, 2 * size), f32),
             pltpu.VMEM((size, size), f32),
             pltpu.VMEM((size, size), f32),
             faces_z, faces_y, faces_z, faces_y, owned, pieces, owned,
             pltpu.VMEM((2, early, wide), f32),
+            pltpu.VMEM((*(2,) * turns, nfar, piece, size), f32),
             pltpu.SemaphoreType.DMA((2, cells // step)),
             pltpu.SemaphoreType.DMA((4,)),
-            ys, ys,
+            ys, ys, every, every,
             near, near, far, far, far, far, near, near,
             zs, zs, ys, ys, every, every, every, every,
         ],

time: 86 us -> 82.6 us (0.960)
  Pallas kernels: 84.5 us -> 81.1 us
    pallas_call x1, Pallas kernels: 82.9 us -> 79.5 us  [on_device(): pl.pallas_call(functools.partial(whole_kernel, nslab, nsub, points, 2), o...]
where the time goes in v5:
time: 82.6 us; the launch traced here: 82.3 us
  Pallas kernels  81.1 us (98%)
  between operations  1.29 us (2%)
    pallas_call x1, Pallas kernels, on_device(): pl.pallas_call(functools.partial(whole_kernel, nslab, nsub, points, 2), o...  79.5 us

profile of v5, /device:TPU:0, one launch (start us, length us, event | category | flops | bytes accessed | tf_op | source)
XLA Modules:
  0.0 82.3 jit_solution(12896540969111227727)
XLA Ops:
  1.3 79.5 %shard_map.102.raw_ref = f32[272,128]{1,0:T(8,128)} custom-call(f32[4096,512]{1,0:T(8,128)} %bitcast.3, f32[4096,512]{1,0:T(8,128)} %bitcast.4, f32[4,1024]{1,0:T(4,128)} %refs_2_.1, f32[4,4,1024]{2,1,0:T(4,128)} %refs_3_.1, f32[4,4,1024]{2,1,0:T(4,128)} %refs_4_.1, f32[512,128]{1,0:T(8,128)} %refs_5_.1), custom_call_target="tpu_custom_call" | custom-call | tf_op jit(solution)/shard_map/pallas_call | solution.py:714
  80.8 1.6 %shard_map.103 = (f32[128,128]{1,0:T(8,128)}, f32[128,128]{1,0:T(8,128)}, f32[4,128]{1,0:T(4,128)}, f32[4,128]{1,0:T(4,128)}) custom-call(s32[1]{0:T(128)S(6)} %copy.11.order_ref, f32[272,128]{1,0:T(8,128)} %shard_map.102.raw_ref), custom_call_target="tpu_custom_call" | custom-call | tf_op jit(solution)/shard_map/pallas_call | solution.py:768
